TPU v7x, 256 devices: a whole 4x4x8 slice. The times are simulated.
256 devices in a mesh: seq: 64 (over x, z, core), head: 4 (over y).
Axes of the slice: x: 4, y: 4, z: 8, core: 2. Of those that a mesh axis runs over, the one named last changes fastest.
Arguments:
- x_in: bfloat16 [65536, 4096], P('seq', 'head'), may hold values from -6 to 6
- z_gate: bfloat16 [65536, 4096], P('seq', 'head'), may hold values from -6 to 6
- b_in: bfloat16 [65536, 128], P('seq', 'head'), may hold values from -2 to 2
- c_in: bfloat16 [65536, 128], P('seq', 'head'), may hold values from -2 to 2
- dt_raw: float32 [65536, 64], P('seq', 'head'), may hold values from -4 to 4
- decay_rate: float32 [64], P('head'), may hold values from 7.6293945e-06 to 0.05, as said below
- skip_gain: float32 [64], P('head'), may hold values from 0.5 to 1.5
- norm_gain: float32 [4096], P('head'), may hold values from 0.1 to 1.9
- w_out: bfloat16 [4096, 2560], P('head'), may hold values from -0.09375 to 0.09375
- doc_lengths: int32 [32], replicated, may hold values from 1 to 16384, 65536 in all
Outputs:
- mixed: bfloat16 [65536, 2560], P(('seq', 'head'))
Inputs may be any that keep to these rules, and one draw needn't show every extreme that they name: `decay_rate`: every head's rate lies in the range. `doc_lengths`: they sum to 65536; the longest is exactly 16384.
All inputs are finite; a program needn't handle non-finite values.
Results may differ from a plain program's by a relative error of at most 0.018.
Values may be sent and summed in bfloat16 or wider, within the bound.
A program may use at most 128 MiB of HBM per device.

v0:
```python
import jax
import jax.numpy as jnp
from jax import lax
from jax.sharding import Mesh
from jax.sharding import PartitionSpec as P

SPAN = 256
SEQ = ("seq_0", "seq_1", "seq_2")
SEQ_HEAD = ("seq_0", "seq_1", "seq_2", "head")


norm_eps = 1e-05


def nothing_yet(x, identity):
    return jax.tree.map(
        lambda part, zero: jnp.zeros_like(part) + jnp.asarray(zero, part.dtype), x, identity
    )


def entering(x, axes, combine, identity):
    before = start = nothing_yet(x, identity)
    subtotal = x
    for axis in reversed(axes):
        length, place = (lax.axis_size(axis), lax.axis_index(axis))
        pieces = jax.tree.map(
            lambda part, kind: lax.all_gather(part.astype(kind), axis),
            subtotal,
            (jnp.bfloat16, jnp.bfloat16),
        )
        inside, subtotal = (start, start)
        for k in range(length):
            passed = k < place
            subtotal = combine(
                subtotal, jax.tree.map(lambda part, own: part[k].astype(own.dtype), pieces, x)
            )
            inside = jax.tree.map(lambda new, old: jnp.where(passed, new, old), subtotal, inside)
        before = combine(inside, before)
    return before


def on_device(
    x_in, z_gate, b_in, c_in, dt_raw, decay_rate, skip_gain, norm_gain, w_out, doc_lengths
):
    rows_here, local_width = x_in.shape
    local_heads = dt_raw.shape[1]
    head_size = local_width // local_heads
    head_groups = lax.axis_size("head")
    b_full, c_full = (
        lax.all_gather(b_in, "head", axis=1, tiled=True),
        lax.all_gather(c_in, "head", axis=1, tiled=True),
    )
    state_size = b_full.shape[1]
    spans = rows_here // SPAN
    offset = lax.axis_index(SEQ) * rows_here
    positions = offset + jnp.arange(rows_here, dtype=jnp.int32)
    doc_ends = jnp.cumsum(doc_lengths)
    doc_starts = doc_ends - doc_lengths
    doc_ids = jnp.sum((positions[:, None] >= doc_ends[None, :]).astype(jnp.int32), axis=1)
    start_flags = jnp.any(positions[:, None] == doc_starts[None, :], axis=1).astype(jnp.int32)
    step_size = jax.nn.softplus(dt_raw)
    log_decay = -step_size * decay_rate[None, :]
    inputs = x_in.reshape(spans, SPAN, local_heads, head_size)
    b_blocks = b_full.reshape(spans, SPAN, state_size)
    c_blocks = c_full.reshape(spans, SPAN, state_size)
    step_blocks = step_size.reshape(spans, SPAN, local_heads)
    decay_blocks = log_decay.reshape(spans, SPAN, local_heads)
    id_blocks = doc_ids.reshape(spans, SPAN)
    flag_blocks = start_flags.reshape(spans, SPAN)
    cumulative = jnp.cumsum(decay_blocks, axis=1)
    unreset = (jnp.cumsum(flag_blocks, axis=1) == 0).astype(jnp.float32)
    from_start = jnp.exp(cumulative) * unreset[:, :, None]

    def combine(earlier, latter):
        return (earlier[0] * latter[0], latter[1] + latter[0][:, None, None] * earlier[1])

    local_pos = jnp.arange(SPAN, dtype=jnp.int32)
    causal_mask = local_pos[:, None] >= local_pos[None, :]
    scores = jnp.einsum("cin,cjn->cij", c_blocks, b_blocks, preferred_element_type=jnp.float32)
    same_doc = causal_mask[None] & (id_blocks[:, :, None] == id_blocks[:, None, :])
    cum_heads = jnp.swapaxes(cumulative, 1, 2)
    differ = cum_heads[:, :, :, None] - cum_heads[:, :, None, :]
    decay_table = jnp.exp(jnp.where(same_doc[:, None], differ, -jnp.inf))
    weights = (
        scores[:, None] * decay_table * jnp.swapaxes(step_blocks, 1, 2)[:, :, None, :]
    ).astype(jnp.bfloat16)
    y_local = jnp.einsum("chij,cjhp->cihp", weights, inputs, preferred_element_type=jnp.float32)
    to_end = jnp.exp(cumulative[:, -1:, :] - cumulative) * (id_blocks == id_blocks[:, -1:])[
        :, :, None
    ].astype(jnp.float32)
    scaled = (inputs * (to_end * step_blocks)[:, :, :, None]).astype(jnp.bfloat16)
    block_states = jnp.einsum(
        "cjhp,cjn->chpn", scaled, b_blocks, preferred_element_type=jnp.float32
    )
    running = jnp.zeros((local_heads, head_size, state_size), jnp.float32)
    decay_total = jnp.ones((local_heads,), jnp.float32)
    befores = []
    for span_index in range(spans):
        befores.append(running)
        running = from_start[span_index, -1][:, None, None] * running + block_states[span_index]
        decay_total = decay_total * from_start[span_index, -1]
    scanned = entering(
        (decay_total, running), SEQ, combine, (jnp.ones_like(decay_total), jnp.zeros_like(running))
    )
    befores, incoming = (jnp.stack(befores), scanned[1])
    y_inter = (
        jnp.einsum("cin,chpn->cihp", c_blocks.astype(jnp.float32), befores)
        * from_start[:, :, :, None]
    )
    cum_device = jnp.cumsum(log_decay, axis=0)
    unreset_device = (jnp.cumsum(start_flags) == 0).astype(jnp.float32)
    from_device = jnp.exp(cum_device) * unreset_device[:, None]
    y_carry = (
        jnp.einsum("tn,hpn->thp", c_full.astype(jnp.float32), incoming) * from_device[:, :, None]
    )
    y_total = (y_local + y_inter).reshape(rows_here, local_heads, head_size) + y_carry
    y_total = y_total + skip_gain[None, :, None] * x_in.reshape(
        rows_here, local_heads, head_size
    ).astype(jnp.float32)
    gated = y_total.reshape(rows_here, local_width) * jax.nn.silu(z_gate.astype(jnp.float32))
    square_sums = jnp.sum(gated * gated, axis=1)
    normed = (gated * norm_gain[None, :]).astype(jnp.bfloat16)
    own_rows = rows_here // head_groups
    full_width = local_width * head_groups
    all_squares = lax.psum(square_sums, "head")
    row_squares = lax.dynamic_slice_in_dim(
        all_squares, lax.axis_index("head") * own_rows, own_rows, 0
    )
    summed = lax.psum_scatter(
        jnp.dot(normed, w_out, preferred_element_type=jnp.float32).astype(jnp.bfloat16),
        "head",
        scatter_dimension=0,
        tiled=True,
    ).astype(jnp.float32)
    inverse_rms = lax.rsqrt(row_squares / full_width + norm_eps)
    return (summed * inverse_rms[:, None]).astype(jnp.bfloat16)


def solution(mesh):
    finer = Mesh(
        mesh.devices.reshape(4, 8, 2, mesh.shape["head"]), ("seq_0", "seq_1", "seq_2", "head")
    )
    return jax.shard_map(
        on_device,
        mesh=finer,
        in_specs=(
            P(SEQ, "head"),
            P(SEQ, "head"),
            P(SEQ, "head"),
            P(SEQ, "head"),
            P(SEQ, "head"),
            P("head"),
            P("head"),
            P("head"),
            P("head", None),
            P(),
        ),
        out_specs=P(SEQ_HEAD, None),
        check_vma=False,
    )
```

profile of v0, /device:TPU:1, one launch (start us, length us, event | category | flops | bytes accessed | tf_op | source)
XLA Modules:
  0.0 211.0 jit_solution(16979415213806899158)
XLA Ops:
  11.1 2.3 %reduce-window.39 = f32[4,16,2,128]{3,1,2,0:T(8,128)S(1)} reduce-window(f32[4,16,2,128]{3,1,2,0:T(8,128)S(1)} %copy_bitcast_fusion.1, f32[]{:T(128)} %constant.32.clone.1), window={size=1x1x1x128 pad=0_0x0_0x0_0x127_0}, to_apply=%region_2.3 | reduce-window | flops 2080768 | bytes 131076 | tf_op jit(solution)/shard_map/reduce-window.1
  15.0 4.7 %all-gather = bf16[2,1,16]{2,1,0:T(2,128)(2,1)S(1)} all-gather(bf16[1,1,16]{2,1,0:T(2,128)(2,1)S(1)} %copy.115), channel_id=2, replica_groups=mesh['seq_0'=4,'seq_1'=8,'seq_2'=2,'head'=4] {'seq_2'}, dimensions={0}, use_global_device_ids=true | all-gather | bytes 96 | tf_op jit(solution)/shard_map/all_gather | solution.py:27
  19.8 9.6 %all_gather.31 = bf16[1024,128]{0,1:T(8,128)(2,1)S(1)} all-gather(bf16[1024,32]{0,1:T(8,128)(2,1)} %param.12), channel_id=1, replica_groups=mesh['seq_0'=4,'seq_1'=8,'seq_2'=2,'head'=4] {'head'}, dimensions={1}, use_global_device_ids=true | all-gather | bytes 327680 | tf_op jit(solution)/shard_map/all_gather | solution.py:50
  29.5 4.0 %copy.107 = bf16[1024,1024]{0,1:T(8,128)(2,1)} copy(bf16[1024,1024]{1,0:T(8,128)(2,1)} %param.10) | data formatting | bytes 4194304 | tf_op args[0]
  33.5 3.3 %reshape.441 = bf16[4,256,16,64]{1,0,3,2:T(4,128)(2,1)S(1)} reshape(bf16[1024,1024]{0,1:T(8,128)(2,1)} %copy.107) | data formatting | bytes 4194304 | tf_op jit(solution)/shard_map/reshape | solution.py:63
  38.9 5.0 %all_gather.32 = bf16[2,16,64,128]{3,2,1,0:T(8,128)(2,1)S(1)} all-gather(bf16[1,16,64,128]{3,2,1,0:T(8,128)(2,1)S(1)} %get-tuple-element.11), channel_id=1, replica_groups=mesh['seq_0'=4,'seq_1'=8,'seq_2'=2,'head'=4] {'seq_2'}, dimensions={0}, use_global_device_ids=true | all-gather | bytes 786432 | tf_op jit(solution)/shard_map/all_gather | solution.py:27
  45.7 9.4 %all_gather.30 = bf16[1024,128]{0,1:T(8,128)(2,1)S(1)} all-gather(bf16[1024,32]{0,1:T(8,128)(2,1)S(1)} %copy-done.3), channel_id=1, replica_groups=mesh['seq_0'=4,'seq_1'=8,'seq_2'=2,'head'=4] {'head'}, dimensions={1}, use_global_device_ids=true | all-gather | bytes 327680 | tf_op jit(solution)/shard_map/all_gather | solution.py:51
  55.2 15.8 %all-gather.1 = bf16[8,1,16]{2,1,0:T(2,128)(2,1)S(1)} all-gather(bf16[1,1,16]{2,1,0:T(2,128)(2,1)S(1)} %multiply_convert_fusion.8), channel_id=1, replica_groups=mesh['seq_0'=4,'seq_1'=8,'seq_2'=2,'head'=4] {'seq_1'}, dimensions={0}, use_global_device_ids=true | all-gather | bytes 288 | tf_op jit(solution)/shard_map/all_gather | solution.py:27
  72.0 1.3 fusion.158
  73.2 2.8 %fusion.15 = f32[4,16,64,256]{3,2,1,0:T(8,128)} fusion(bf16[4,256,128,1]{2,1,3,0:T(8,128)(2,1)S(1)} %bitcast.319, bf16[1,16,64,128]{3,2,1,0:T(8,128)(2,1)S(1)} %get-tuple-element.12, bf16[1,16,64,128]{3,2,1,0:T(8,128)(2,1)S(1)} %get-tuple-element.13, bf16[1,16,64,128]{3,2,1,0:T(8,128)(2,1)S(1)} %get-tuple-element.14, bf16[4]{0:T(256)(128)(2,1)S(1)} %pad.clone), kind=kOutput, calls=%fused_computation.25 | convolution fusion | flops 270008320 | bytes 5242888 | tf_op jit(solution)/shard_map/cin,chpn->cihp/dot_general | solution.py:107
  76.0 6.7 %all-gather.6.cloned.1.call-done = bf16[8,16,64,128]{3,2,1,0:T(8,128)(2,1)} async-done(((bf16[1,16,64,128]{3,2,1,0:T(8,128)(2,1)}), bf16[8,16,64,128]{3,2,1,0:T(8,128)(2,1)}) %all-gather.6.cloned.1.call-update) | async-done | bytes 2097168 | tf_op jit(solution)/shard_map/all_gather | solution.py:27
  82.7 2.8 %fusion.43 = bf16[1,16,64,128]{3,2,1,0:T(8,128)(2,1)} fusion(f32[16]{0:T(128)S(1)} %bitcast_multiply_fusion.10, f32[16]{0:T(128)S(1)} %get-tuple-element.22, f32[16]{0:T(128)S(1)} %get-tuple-element.23, f32[16]{0:T(128)S(1)} %get-tuple-element.24, f32[16]{0:T(128)S(1)} %get-tuple-element.25, f32[16]{0:T(128)S(1)} %get-tuple-element.26, ...), kind=kLoop, calls=%fused_computation.70 | loop fusion | flops 3145728 | bytes 2359808 | tf_op jit(solution)/shard_map/convert_element_type | solution.py:27
  85.6 9.1 %fusion.14 = f32[4,16,8,8,256]{4,3,2,1,0:T(8,128)} fusion(f32[4,16,64,256]{3,2,1,0:T(8,128)} %fusion.15, f32[4,16,256]{2,1,0:T(8,128)S(1)} %copy-done.5, f32[4,16,256]{2,1,0:T(8,128)S(1)} %copy-done.4, f32[4,256,256]{2,1,0:T(8,128)} %fusion.158, pred[4,256,256]{2,1,0:T(8,128)(4,1)S(1)} %compare_and_fusion, bf16[4,256,16,64]{1,0,3,2:T(4,128)(2,1)} %copy-done.1, ...), kind=kOutput, calls=%fused_computation.20 | convolution fusion | flops 559939584 | bytes 11993088 | tf_op jit(solution)/shard_map/chij,cjhp->cihp/dot_general | solution.py:87
  94.7 7.9 %all-gather.2 = bf16[4,1,16]{2,1,0:T(2,128)(2,1)S(1)} all-gather(bf16[1,1,16]{2,1,0:T(2,128)(2,1)S(1)} %copy-done.24), channel_id=1, replica_groups=mesh['seq_0'=4,'seq_1'=8,'seq_2'=2,'head'=4] {'seq_0'}, dimensions={0}, use_global_device_ids=true | all-gather | bytes 160 | tf_op jit(solution)/shard_map/all_gather | solution.py:27
  102.5 3.1 %copy.119 = f32[1024,1024]{0,1:T(8,128)} copy(bf16[1024,1024]{1,0:T(8,128)(2,1)S(1)} %copy-done) | data formatting | bytes 6291456 | tf_op jit(solution)/shard_map/convert_element_type | solution.py:119
  106.0 4.5 %reduce-window.54 = f32[16,8,128]{2,1,0:T(8,128)S(1)} reduce-window(f32[16,8,128]{2,1,0:T(8,128)S(1)} %bitcast.327, f32[]{:T(128)} %constant.32.clone.1), window={size=1x1x128 pad=0_0x0_0x127_0}, to_apply=%region_7.8 | reduce-window | flops 2080768 | bytes 131076 | tf_op jit(solution)/shard_map/reduce-window.5
  111.0 4.8 %copy.127 = f32[4,16,8,8,256]{4,3,0,2,1:T(8,128)} copy(f32[4,16,8,8,256]{4,3,2,1,0:T(8,128)} %fusion.14) | data formatting | bytes 8388608 | tf_op jit(solution)/shard_map/reshape | solution.py:116
  116.4 8.3 %fusion.12 = f32[1024,16,64]{0,2,1:T(8,128)} fusion(f32[1024,16,64]{0,2,1:T(8,128)} %bitcast.316, f32[1024,16,64]{0,2,1:T(8,128)} %bitcast.315, f32[16]{0:T(128)S(1)} %copy-done.27, f32[1024,16]{0,1:T(8,128)S(1)} %fusion.135, bf16[4,16,64,128]{3,2,1,0:T(8,128)(2,1)} %all-gather.8.cloned.1.call-done, bf16[1024,128]{0,1:T(8,128)(2,1)S(1)} %all_gather.30, ...), kind=kOutput, calls=%fused_computation.17 | convolution fusion | flops 280100864 | bytes 16581710 | tf_op jit(solution)/shard_map/tn,hpn->thp/dot_general | solution.py:114
  124.7 5.5 %copy.120 = f32[1024,1024]{1,0:T(8,128)} copy(f32[1024,1024]{0,1:T(8,128)} %bitcast.317) | data formatting | bytes 8388608 | tf_op jit(solution)/shard_map/reshape | solution.py:120
  130.2 10.7 %convolution_convert_fusion = bf16[1024,2560]{1,0:T(8,128)(2,1)} fusion(bf16[1024,2560]{1,0:T(8,128)(2,1)} %param.18, f32[1024]{0:T(1024)S(1)} %copy-done.28, f32[1024,1024]{1,0:T(8,128)} %copy.120, bf16[1024,1024]{1,0:T(8,128)(2,1)S(1)} %copy-done.2), kind=kOutput, calls=%fused_computation.8 | convolution fusion | flops 5379719168 | bytes 16781312 | tf_op jit(solution)/shard_map/dot_general | solution.py:130
  140.9 3.5 %multiply_reduce_fusion = f32[1024]{0:T(1024)S(1)} fusion(f32[1024,1024]{1,0:T(8,128)} %copy.120, bf16[1024,1024]{1,0:T(8,128)(2,1)S(1)} %copy-done.2), kind=kLoop, calls=%fused_computation.21 | loop fusion | flops 8387584 | bytes 6295552 | tf_op jit(solution)/shard_map/reduce_sum | solution.py:121
  144.5 8.5 %psum.7 = f32[1024]{0:T(1024)S(1)} all-reduce(f32[1024]{0:T(1024)S(1)} %multiply_reduce_fusion), channel_id=1, replica_groups=mesh['seq_0'=4,'seq_1'=8,'seq_2'=2,'head'=4] {'head'}, use_global_device_ids=true, to_apply=%region_13.14 | all-reduce | flops 1024 | bytes 8192 | tf_op jit(solution)/shard_map/psum | solution.py:125
  153.0 48.8 %reduce-scatter.2.cloned.1.call-done = bf16[256,2560]{1,0:T(8,128)(2,1)} async-done(((bf16[1024,2560]{1,0:T(8,128)(2,1)}), bf16[256,2560]{1,0:T(8,128)(2,1)}) %reduce-scatter.2.cloned.1.call-update) | async-done | bytes 1310736 | tf_op jit(solution)/shard_map/reduce_scatter | solution.py:129
  201.8 2.7 %multiply_convert_fusion.4 = bf16[256,2560]{1,0:T(8,128)(2,1)} fusion(bf16[256,2560]{1,0:T(8,128)(2,1)} %reduce-scatter.2.cloned.1.call-done, f32[256]{0:T(256)S(1)} %add_rsqrt_fusion), kind=kLoop, calls=%fused_computation.24 | loop fusion | flops 1966080 | bytes 2622464 | tf_op jit(solution)/shard_map/convert_element_type | solution.py:136
  (133 shorter events, 12.7 us)
Async XLA Ops:
  6.5 76.1 %all-gather.6.cloned.1.call-start = ((), (), s32[]{:S(2)}) async-start(), calls=%async_computation.1 | async-start | bytes 2359296 | tf_op jit(solution)/shard_map/all_gather | solution.py:27
  19.7 35.5 %copy-start.25 = (bf16[2,1,16]{2,1,0:T(2,128)(2,1)}, bf16[2,1,16]{2,1,0:T(2,128)(2,1)S(1)}, u32[]{:S(2)}) copy-start(bf16[2,1,16]{2,1,0:T(2,128)(2,1)S(1)} %all-gather) | copy-start | bytes 196
  19.7 24.3 %copy-start.18 = (f32[16]{0:T(128)}, f32[16]{0:T(128)S(1)}, u32[]{:S(2)}) copy-start(f32[16]{0:T(128)S(1)} %fusion.145) | copy-start | bytes 196
  19.7 24.2 %copy-start.20 = (f32[16]{0:T(128)}, f32[16]{0:T(128)S(1)}, u32[]{:S(2)}) copy-start(f32[16]{0:T(128)S(1)} %bitcast_multiply_fusion.12) | copy-start | bytes 196
  37.9 7.8 %copy-start.3 = (bf16[1024,32]{0,1:T(8,128)(2,1)S(1)}, bf16[1024,32]{0,1:T(8,128)(2,1)}, u32[]{:S(2)}) copy-start(bf16[1024,32]{0,1:T(8,128)(2,1)} %param.13) | copy-start | bytes 196612
  45.0 71.4 %all-gather.8.cloned.1.call-start = ((), (), s32[]{:S(2)}) async-start(), calls=%async_computation.2 | async-start | bytes 1310720 | tf_op jit(solution)/shard_map/all_gather | solution.py:27
  71.1 11.6 %copy-start.22 = (f32[16]{0:T(128)}, f32[16]{0:T(128)S(1)}, u32[]{:S(2)}) copy-start(f32[16]{0:T(128)S(1)} %bitcast_multiply_fusion.10) | copy-start | bytes 196
  71.6 11.0 %copy-start.6 = (f32[16]{0:T(128)}, f32[16]{0:T(128)S(1)}, u32[]{:S(2)}) copy-start(f32[16]{0:T(128)S(1)} %get-tuple-element.22) | copy-start | bytes 196
  71.7 11.0 %copy-start.8 = (f32[16]{0:T(128)}, f32[16]{0:T(128)S(1)}, u32[]{:S(2)}) copy-start(f32[16]{0:T(128)S(1)} %get-tuple-element.23) | copy-start | bytes 196
  71.7 11.0 %copy-start.10 = (f32[16]{0:T(128)}, f32[16]{0:T(128)S(1)}, u32[]{:S(2)}) copy-start(f32[16]{0:T(128)S(1)} %get-tuple-element.24) | copy-start | bytes 196
  71.7 11.0 %copy-start.12 = (f32[16]{0:T(128)}, f32[16]{0:T(128)S(1)}, u32[]{:S(2)}) copy-start(f32[16]{0:T(128)S(1)} %get-tuple-element.25) | copy-start | bytes 196
  71.7 11.0 %copy-start.14 = (f32[16]{0:T(128)}, f32[16]{0:T(128)S(1)}, u32[]{:S(2)}) copy-start(f32[16]{0:T(128)S(1)} %get-tuple-element.26) | copy-start | bytes 196
  71.7 11.0 %copy-start.16 = (f32[16]{0:T(128)}, f32[16]{0:T(128)S(1)}, u32[]{:S(2)}) copy-start(f32[16]{0:T(128)S(1)} %get-tuple-element.27) | copy-start | bytes 196
  73.2 12.3 %copy-start.4 = (f32[4,16,256]{2,1,0:T(8,128)S(1)}, f32[4,16,256]{2,1,0:T(8,128)}, u32[]{:S(2)}) copy-start(f32[4,16,256]{2,1,0:T(8,128)} %get-tuple-element.15) | copy-start | bytes 196612
  73.2 12.3 %copy-start.5 = (f32[4,16,256]{2,1,0:T(8,128)S(1)}, f32[4,16,256]{2,1,0:T(8,128)}, u32[]{:S(2)}) copy-start(f32[4,16,256]{2,1,0:T(8,128)} %copy.106) | copy-start | bytes 196612
  85.5 116.3 %reduce-scatter.2.cloned.1.call-start = ((), (), s32[]{:S(2)}) async-start(), calls=%async_computation.3 | async-start | bytes 6553600 | tf_op jit(solution)/shard_map/reduce_scatter | solution.py:129
  85.6 9.1 %copy-start.24 = (bf16[1,1,16]{2,1,0:T(2,128)(2,1)S(1)}, bf16[1,1,16]{2,1,0:T(2,128)(2,1)}, u32[]{:S(2)}) copy-start(bf16[1,1,16]{2,1,0:T(2,128)(2,1)} %fusion.144) | copy-start | bytes 100
  85.6 16.9 %copy-start = (bf16[1024,1024]{1,0:T(8,128)(2,1)S(1)}, bf16[1024,1024]{1,0:T(8,128)(2,1)}, u32[]{:S(2)}) copy-start(bf16[1024,1024]{1,0:T(8,128)(2,1)} %param.10) | copy-start | bytes 6291460
  110.9 5.4 %copy-start.11 = (f32[16]{0:T(128)S(1)}, f32[16]{0:T(128)}, u32[]{:S(2)}) copy-start(f32[16]{0:T(128)} %copy-done.10) | copy-start | bytes 196
  111.0 5.4 %copy-start.13 = (f32[16]{0:T(128)S(1)}, f32[16]{0:T(128)}, u32[]{:S(2)}) copy-start(f32[16]{0:T(128)} %copy-done.12) | copy-start | bytes 196
  111.0 5.4 %copy-start.15 = (f32[16]{0:T(128)S(1)}, f32[16]{0:T(128)}, u32[]{:S(2)}) copy-start(f32[16]{0:T(128)} %copy-done.14) | copy-start | bytes 196
  111.0 5.4 %copy-start.17 = (f32[16]{0:T(128)S(1)}, f32[16]{0:T(128)}, u32[]{:S(2)}) copy-start(f32[16]{0:T(128)} %copy-done.16) | copy-start | bytes 196
  124.7 5.5 %copy-start.2 = (bf16[1024,1024]{1,0:T(8,128)(2,1)S(1)}, bf16[1024,1024]{1,0:T(8,128)(2,1)}, u32[]{:S(2)}) copy-start(bf16[1024,1024]{1,0:T(8,128)(2,1)} %param.11) | copy-start | bytes 6291460
  124.7 5.5 %copy-start.28 = (f32[1024]{0:T(1024)S(1)}, f32[1024]{0:T(1024)}, u32[]{:S(2)}) copy-start(f32[1024]{0:T(1024)} %param.17) | copy-start | bytes 12292
  (8 other events, 39.4 us)
Sparse Core Ops, SparseCore 0:
  45.1 37.5 all-gather.5
  85.6 27.4 all-gather.7
  141.0 60.7 reduce-scatter.1
where the time goes:
time: 212 us; the launch traced here: 211 us
  blocking collectives  60.8 us (29%)
  waiting for transfers between devices  55.5 us (26%)
  matrix products  32.8 us (15%)
  other arithmetic  24.1 us (11%)
  local copies, waits for them, and re-layouts  24.1 us (11%)
  between operations  13.6 us (6%)
    reduce_scatter x1, waiting for transfers between devices, on_device(): lax.psum_scatter(jnp.dot(normed, w_out, preferred_element_type=jnp.float3...  48.8 us
    all_gather x4, blocking collectives, entering(): lax.all_gather(part.astype(kind), axis)  33.4 us
    dot_general x1, matrix products, on_device(): jnp.dot(normed, w_out, preferred_element_type=jnp.float32)  10.7 us
    all_gather x1, blocking collectives, on_device(): lax.all_gather(b_in, 'head', axis=1, tiled=True)  9.58 us
    all_gather x1, blocking collectives, on_device(): lax.all_gather(c_in, 'head', axis=1, tiled=True)  9.36 us
    another operation x11, other arithmetic  9.28 us
    dot_general x1, matrix products, on_device(): jnp.einsum('chij,cjhp->cihp', weights, inputs, preferred_element_type=jnp...  9.08 us
    psum x1, blocking collectives, on_device(): all_squares = lax.psum(square_sums, 'head')  8.49 us
  transfers between devices with their start and end apart: 3, of which 2 were waited for; matrix products, arithmetic and copies ran while one was open for 15% of the time, Pallas kernels for 0%

commit v1 on v0

v1 whole, which is shorter than its diff:
```python
import functools

import jax
import jax.numpy as jnp
from jax import lax
from jax.experimental import pallas as pl
from jax.experimental.pallas import tpu as pltpu
from jax.sharding import PartitionSpec as P

SPAN = 256
NORM_EPS = 1e-05
MESH = pl.DeviceIdType.MESH
F32 = jnp.float32
BF16 = jnp.bfloat16


def pieces(v, terms):
    out = []
    for _ in range(terms):
        part = v.astype(BF16)
        out.append(part)
        v = v - part.astype(F32)
    return out


def expand(v, spread, terms=2):
    total = None
    for part in pieces(v, terms):
        term = jnp.dot(part, spread, preferred_element_type=F32)
        total = term if total is None else total + term
    return total


def iota(shape, dim):
    return lax.broadcasted_iota(jnp.int32, shape, dim)


def layer_kernel(
    sizes,
    bc_ref, dt_ref, rate_ref, skip_ref, gain_ref, docs_ref, x_hbm, z_hbm, w_hbm,
    out_ref,
    x_ref, z_ref, w_ref, bt_ref, ct_ref, xf_ref, e_ref, rows_ref, before_ref, ur_ref, as_ref,
    state_ref, decay_ref, got_state, got_decay, line_ref, got_line, back_ref, inc_ref, norm_ref,
    sq_ref, got_sq, send_r, got_r, send_l, got_l,
    in_sem, bc_send, bc_recv, st_send, st_recv, dc_send, dc_recv, ln_send, ln_recv, bk_send, bk_recv,
    sq_send, sq_recv, r_send, r_recv, l_send, l_recv,
):
    n_head, n_seq, line = sizes
    rows, width = x_ref.shape
    heads = dt_ref.shape[1]
    head_size = width // heads
    state_size = bt_ref.shape[0]
    piece = bc_ref.shape[0] // 2
    spans = rows // SPAN
    me, seq = lax.axis_index("head"), lax.axis_index("seq")
    at_line, place = seq // line, seq % line
    first = seq - place
    half = width // 2
    part = state_size * 2 // line

    def load(i, src, dst):
        return pltpu.make_async_copy(src, dst, in_sem.at[i])

    loads = [load(0, x_hbm, x_ref), load(1, z_hbm, z_ref), load(2, w_hbm, w_ref)]
    for one in loads:
        one.start()

    barrier = pltpu.get_barrier_semaphore()
    for k in range(1, n_head):
        pl.semaphore_signal(barrier, inc=1, device_id={"head": (me + k) % n_head}, device_id_type=MESH)

    @pl.loop(1, line)
    def _(k):
        pl.semaphore_signal(
            barrier, inc=1, device_id={"seq": first + (place + k) % line}, device_id_type=MESH
        )

    for step in (line, n_seq - line):
        pl.semaphore_signal(barrier, inc=1, device_id={"seq": (seq + step) % n_seq}, device_id_type=MESH)
    pl.semaphore_wait(barrier, n_head - 1 + line - 1 + 2)

    def bc_copy(k, what, owner):
        dst = (bt_ref, ct_ref)[what].at[pl.ds(pl.multiple_of(owner * piece, piece), piece), :]
        return pltpu.make_async_remote_copy(
            src_ref=bc_ref.at[pl.ds(what * piece, piece), :],
            dst_ref=dst,
            send_sem=bc_send.at[what, k],
            recv_sem=bc_recv.at[what, owner],
            device_id={"head": (me + k) % n_head},
            device_id_type=MESH,
        )

    for what in range(2):
        for k in range(1, n_head):
            bc_copy(k, what, me).start()
        mine = pl.ds(pl.multiple_of(me * piece, piece), piece)
        (bt_ref, ct_ref)[what][mine, :] = bc_ref[what * piece : (what + 1) * piece, :]

    n_docs = docs_ref.shape[1]
    lengths = jnp.broadcast_to(docs_ref[...].astype(F32), (n_docs, n_docs))
    up, across = iota((n_docs, n_docs), 0), iota((n_docs, n_docs), 1)
    ends_col = jnp.sum(jnp.where(across <= up, lengths, 0.0), axis=1, keepdims=True)
    lengths_col = jnp.sum(jnp.where(across == up, lengths, 0.0), axis=1, keepdims=True)
    ends_row = jnp.sum(
        jnp.where(up <= across, jnp.broadcast_to(lengths_col, (n_docs, n_docs)), 0.0), axis=0, keepdims=True
    )

    def id_of(position):
        return jnp.sum(jnp.where(position >= ends_row, 1.0, 0.0), axis=1, keepdims=True)

    def ids_of(s):
        start = seq * rows + s * SPAN
        col = id_of((start + iota((SPAN, 1), 0)).astype(F32))
        row = jnp.sum(
            jnp.where((start + iota((1, SPAN), 1)).astype(F32) >= ends_col, 1.0, 0.0), axis=0, keepdims=True
        )
        ahead = start - 1 + iota((1, 1), 0)
        previous = id_of(ahead.astype(F32)) - jnp.where(ahead < 0, 1.0, 0.0)
        last = id_of((start + SPAN - 1 + iota((1, 1), 0)).astype(F32))
        return col, row, previous, last

    spread = (iota((heads, width), 1) // head_size == iota((heads, width), 0)).astype(BF16)
    below = (iota((SPAN, SPAN), 0) >= iota((SPAN, SPAN), 1)).astype(BF16)

    loads[0].wait()

    def scale_span(s, device_decay):
        at = pl.ds(pl.multiple_of(s * SPAN, SPAN), SPAN)
        raw = dt_ref[at, :]
        step = jnp.maximum(raw, 0.0) + jnp.log(1.0 + jnp.exp(-jnp.abs(raw)))
        cum = None
        for term in pieces(-step * rate_ref[...], 3):
            sums = jnp.dot(below, term, preferred_element_type=F32)
            cum = sums if cum is None else cum + sums
        middle = 0.5 * cum[SPAN - 1 : SPAN, :]
        e_ref[at, :] = jnp.exp(cum - middle)
        forward = step * jnp.exp(middle - cum)
        xf_ref[at, :] = (x_ref[at, :].astype(F32) * expand(forward, spread)).astype(BF16)
        _, _, previous, last = ids_of(s)
        to_middle = jnp.exp(middle)
        total = jnp.exp(2.0 * middle) * jnp.where(last == previous, 1.0, 0.0)
        both = jnp.concatenate(
            [jnp.broadcast_to(to_middle, (8, heads)), jnp.broadcast_to(total, (8, heads))], axis=0
        )
        rows_ref[pl.ds(pl.multiple_of(s * 16, 16), 16), :] = expand(both, spread, 3)
        return device_decay * total

    device_decay = lax.fori_loop(0, spans, scale_span, jnp.ones((1, heads), F32))
    decay_ref[...] = jnp.zeros_like(decay_ref)
    decay_ref[:, :heads] = jnp.broadcast_to(device_decay, (8, heads))

    def line_peer(k):
        return {"seq": first + (place + k) % line}

    def from_peer(k):
        return (place + line - k) % line

    def decay_copy(k, owner):
        return pltpu.make_async_remote_copy(
            src_ref=decay_ref,
            dst_ref=got_decay.at[owner],
            send_sem=dc_send.at[k],
            recv_sem=dc_recv.at[owner],
            device_id=line_peer(k),
            device_id_type=MESH,
        )

    @pl.loop(1, line)
    def _(k):
        decay_copy(k, place).start()

    got_decay[place] = decay_ref[...]

    for k in range(1, n_head):
        bc_copy(k, 0, (me + n_head - k) % n_head).wait_recv()

    def state_span(s, running):
        at = pl.ds(pl.multiple_of(s * SPAN, SPAN), SPAN)
        before_ref[s] = running
        _, row, _, last = ids_of(s)
        kept = jnp.where(row == last, bt_ref[:, at].astype(F32), 0.0).astype(BF16)
        sums = jnp.dot(kept, xf_ref[at, :], preferred_element_type=F32)
        base = pl.multiple_of(s * 16, 16)
        return rows_ref[pl.ds(base + 8, 1), :] * running + sums * rows_ref[pl.ds(base, 1), :]

    final = lax.fori_loop(0, spans, state_span, jnp.zeros((state_size, width), F32))
    state_ref[...] = final.astype(BF16)

    def own_part(t):
        return (
            pl.ds(pl.multiple_of((t // 2) * part, part), part),
            pl.ds(pl.multiple_of((t % 2) * half, half), half),
        )

    def state_copy(k, owner):
        to = (place + k) % line
        return pltpu.make_async_remote_copy(
            src_ref=state_ref.at[own_part(to)],
            dst_ref=got_state.at[owner],
            send_sem=st_send.at[k],
            recv_sem=st_recv.at[owner],
            device_id=line_peer(k),
            device_id_type=MESH,
        )

    @pl.loop(1, line)
    def _(k):
        state_copy(k, place).start()

    got_state[place] = state_ref[own_part(place)]

    for k in range(1, n_head):
        bc_copy(k, 1, (me + n_head - k) % n_head).wait_recv()
    loads[1].wait()
    skip_row = expand(jnp.broadcast_to(skip_ref[...], (8, heads)), spread, 3)[:1, :]

    @pl.loop(0, spans)
    def _(s):
        at = pl.ds(pl.multiple_of(s * SPAN, SPAN), SPAN)
        col, row, previous, _ = ids_of(s)
        c_here = ct_ref[:, at].T
        scores = jnp.dot(c_here, bt_ref[:, at], preferred_element_type=F32)
        seen = (col == row) & (iota((SPAN, SPAN), 0) >= iota((SPAN, SPAN), 1))
        scores = jnp.where(seen, scores, 0.0).astype(BF16)
        local = jnp.dot(scores, xf_ref[at, :], preferred_element_type=F32)
        inter = jnp.dot(c_here, before_ref[s].astype(BF16), preferred_element_type=F32)
        base = pl.multiple_of(s * 16, 16)
        out_of_middle = expand(e_ref[at, :], spread)
        from_start = rows_ref[pl.ds(base, 1), :] * jnp.where(col == previous, 1.0, 0.0)
        gate = z_ref[at, :].astype(F32)
        gate = gate / (1.0 + jnp.exp(-gate))
        y = out_of_middle * (local + from_start * inter) + skip_row * x_ref[at, :].astype(F32)
        ur_ref[at, :] = y * gate
        as_ref[at, :] = out_of_middle * from_start * gate

    @pl.loop(1, line)
    def _(k):
        decay_copy(k, from_peer(k)).wait_recv()

    @pl.loop(1, line)
    def _(k):
        state_copy(k, from_peer(k)).wait_recv()

    lanes = iota((128, half), 1) + (place % 2) * half
    spread_here = (lanes // head_size == iota((128, half), 0)).astype(BF16)
    decays = expand(got_decay[...].reshape(line * 8, 128), spread_here, 3)
    inside, inc = [], jnp.zeros((part, half), F32)
    for d in range(line):
        inside.append(inc)
        inc = decays[8 * d : 8 * d + 1, :] * inc + got_state[d].astype(F32)
    line_ref[...] = inc
    line_copy = pltpu.make_async_remote_copy(
        src_ref=line_ref,
        dst_ref=got_line,
        send_sem=ln_send,
        recv_sem=ln_recv,
        device_id={"seq": (seq + line) % n_seq},
        device_id_type=MESH,
    )
    line_copy.start()
    line_copy.wait_recv()
    factor = jnp.where(at_line + iota((1, half), 0) > 0, 1.0, 0.0)
    earlier = got_line[...]
    for d in range(line):
        back_ref[d] = (inside[d] + factor * earlier).astype(BF16)
        factor = factor * decays[8 * d : 8 * d + 1, :]

    def back_copy(k, owner):
        return pltpu.make_async_remote_copy(
            src_ref=back_ref.at[(place + k) % line],
            dst_ref=inc_ref.at[own_part(owner)],
            send_sem=bk_send.at[k],
            recv_sem=bk_recv.at[owner],
            device_id=line_peer(k),
            device_id_type=MESH,
        )

    @pl.loop(1, line)
    def _(k):
        back_copy(k, place).start()

    inc_ref[own_part(place)] = back_ref[place]

    loads[2].wait()

    @pl.loop(1, line)
    def _(k):
        back_copy(k, from_peer(k)).wait_recv()

    def finish(block):
        at = pl.ds(pl.multiple_of(block * SPAN, SPAN), SPAN)
        before = jnp.ones((1, width), F32)
        for s in range(spans - 1):
            decay = rows_ref[16 * s + 8 : 16 * s + 9, :]
            before = jnp.where(s + iota((1, width), 0) < block, before * decay, before)
        carried = (inc_ref[...].astype(F32) * before).astype(BF16)
        inter = jnp.dot(ct_ref[:, at].T, carried, preferred_element_type=F32)
        gated = ur_ref[at, :] + as_ref[at, :] * inter
        norm_ref[at, :] = (gated * gain_ref[...]).astype(BF16)
        squares = gated * gated
        folded = squares[:, :128]
        for j in range(1, width // 128):
            folded = folded + squares[:, 128 * j : 128 * (j + 1)]
        row = jnp.sum(folded.T, axis=0, keepdims=True)
        sq_ref[block] = jnp.broadcast_to(row, (8, SPAN))

    def square_copy(k, owner):
        return pltpu.make_async_remote_copy(
            src_ref=sq_ref.at[(me + k) % n_head],
            dst_ref=got_sq.at[owner],
            send_sem=sq_send.at[k],
            recv_sem=sq_recv.at[owner],
            device_id={"head": (me + k) % n_head},
            device_id_type=MESH,
        )

    out_width = out_ref.shape[1]
    parts, cut = got_r.shape[1], got_r.shape[3]

    def product(block, column):
        return jnp.dot(
            norm_ref[pl.ds(pl.multiple_of(block * SPAN, SPAN), SPAN), :],
            w_ref[:, pl.ds(pl.multiple_of(column, cut), cut)],
            preferred_element_type=F32,
        )

    def right_copy(step, j):
        return pltpu.make_async_remote_copy(
            src_ref=send_r.at[step, j],
            dst_ref=got_r.at[step, j],
            send_sem=r_send.at[step, j],
            recv_sem=r_recv.at[step, j],
            device_id={"head": (me + 1) % n_head},
            device_id_type=MESH,
        )

    def left_copy(step, j):
        return pltpu.make_async_remote_copy(
            src_ref=send_l.at[step, j],
            dst_ref=got_l.at[step, j],
            send_sem=l_send.at[step, j],
            recv_sem=l_recv.at[step, j],
            device_id={"head": (me + n_head - 1) % n_head},
            device_id_type=MESH,
        )

    ahead, behind = (me + n_head - 1) % n_head, (me + 1) % n_head
    finish(ahead)

    @pl.loop(0, parts)
    def _(j):
        send_r[0, j] = product(ahead, j * cut).astype(BF16)
        right_copy(0, j).start()

    finish(behind)

    @pl.loop(0, parts)
    def _(j):
        send_l[0, j] = product(behind, out_width // 2 + j * cut).astype(BF16)
        left_copy(0, j).start()

    for k in range(2, n_head):
        finish((me + k) % n_head) if k < n_head - 1 else finish(me)
    for k in range(1, n_head):
        square_copy(k, me).start()

    for step in range(1, n_head - 1):
        block_r, block_l = (me + 2 * n_head - 1 - step) % n_head, (me + 1 + step) % n_head

        @pl.loop(0, parts)
        def _(j):
            own = product(block_r, j * cut)
            right_copy(step - 1, j).wait_recv()
            send_r[step, j] = (own + got_r[step - 1, j].astype(F32)).astype(BF16)
            right_copy(step, j).start()
            own = product(block_l, out_width // 2 + j * cut)
            left_copy(step - 1, j).wait_recv()
            send_l[step, j] = (own + got_l[step - 1, j].astype(F32)).astype(BF16)
            left_copy(step, j).start()

    total = sq_ref[me]
    for k in range(1, n_head):
        owner = (me + n_head - k) % n_head
        square_copy(k, owner).wait_recv()
        total = total + got_sq[owner]
    inverse_rms = lax.rsqrt(total / (width * n_head) + NORM_EPS).T[:, :1]

    @pl.loop(0, parts)
    def _(j):
        last = n_head - 2
        own = product(me, j * cut)
        right_copy(last, j).wait_recv()
        own = (own + got_r[last, j].astype(F32)) * inverse_rms
        out_ref[:, pl.ds(pl.multiple_of(j * cut, cut), cut)] = own.astype(BF16)
        column = out_width // 2 + j * cut
        own = product(me, column)
        left_copy(last, j).wait_recv()
        own = (own + got_l[last, j].astype(F32)) * inverse_rms
        out_ref[:, pl.ds(pl.multiple_of(column, cut), cut)] = own.astype(BF16)

    for k in range(1, n_head):
        for what in range(2):
            bc_copy(k, what, me).wait_send()
        square_copy(k, me).wait_send()

    @pl.loop(1, line)
    def _(k):
        decay_copy(k, place).wait_send()
        state_copy(k, place).wait_send()
        back_copy(k, place).wait_send()

    line_copy.wait_send()
    for step in range(n_head - 1):

        @pl.loop(0, parts)
        def _(j):
            right_copy(step, j).wait_send()
            left_copy(step, j).wait_send()


def on_device(sizes, x_in, z_gate, b_in, c_in, dt_raw, decay_rate, skip_gain, norm_gain, w_out, doc_lengths):
    n_head, n_seq, line = sizes
    rows, width = x_in.shape
    heads = dt_raw.shape[1]
    out_width = w_out.shape[1]
    state_size = b_in.shape[1] * n_head
    spans = rows // SPAN
    bc = jnp.concatenate([b_in, c_in], axis=1).T
    part, half = state_size * 2 // line, width // 2
    parts = 5
    cut = out_width // 2 // parts
    ring = (n_head - 1, parts, rows // n_head, cut)
    vmem, anywhere = pl.BlockSpec(memory_space=pltpu.VMEM), pl.BlockSpec(memory_space=pl.ANY)
    dma = pltpu.SemaphoreType.DMA
    return pl.pallas_call(
        functools.partial(layer_kernel, sizes),
        out_shape=jax.ShapeDtypeStruct((rows // n_head, out_width), BF16),
        in_specs=[vmem] * 6 + [anywhere] * 3,
        out_specs=vmem,
        scratch_shapes=[
            pltpu.VMEM((rows, width), BF16),
            pltpu.VMEM((rows, width), BF16),
            pltpu.VMEM(w_out.shape, BF16),
            pltpu.VMEM((state_size, rows), BF16),
            pltpu.VMEM((state_size, rows), BF16),
            pltpu.VMEM((rows, width), BF16),
            pltpu.VMEM((rows, heads), F32),
            pltpu.VMEM((spans * 16, width), F32),
            pltpu.VMEM((spans, state_size, width), F32),
            pltpu.VMEM((rows, width), F32),
            pltpu.VMEM((rows, width), F32),
            pltpu.VMEM((state_size, width), BF16),
            pltpu.VMEM((8, 128), F32),
            pltpu.VMEM((line, part, half), BF16),
            pltpu.VMEM((line, 8, 128), F32),
            pltpu.VMEM((part, half), F32),
            pltpu.VMEM((part, half), F32),
            pltpu.VMEM((line, part, half), BF16),
            pltpu.VMEM((state_size, width), BF16),
            pltpu.VMEM((rows, width), BF16),
            pltpu.VMEM((n_head, 8, SPAN), F32),
            pltpu.VMEM((n_head, 8, SPAN), F32),
            pltpu.VMEM(ring, BF16),
            pltpu.VMEM(ring, BF16),
            pltpu.VMEM(ring, BF16),
            pltpu.VMEM(ring, BF16),
            dma((3,)),
            dma((2, n_head)),
            dma((2, n_head)),
            dma((line,)),
            dma((line,)),
            dma((line,)),
            dma((line,)),
            dma,
            dma,
            dma((line,)),
            dma((line,)),
            dma((n_head,)),
            dma((n_head,)),
            dma((n_head - 1, parts)),
            dma((n_head - 1, parts)),
            dma((n_head - 1, parts)),
            dma((n_head - 1, parts)),
        ],
        compiler_params=pltpu.CompilerParams(
            collective_id=0, has_side_effects=True, vmem_limit_bytes=60 * 1024 * 1024
        ),
        name="ssd_layer",
    )(
        bc,
        dt_raw,
        decay_rate[None, :],
        skip_gain[None, :],
        norm_gain[None, :],
        doc_lengths[None, :],
        x_in,
        z_gate,
        w_out,
    )


def solution(mesh):
    sizes = (mesh.shape["head"], mesh.shape["seq"], 16)
    rows = P("seq", "head")
    return jax.shard_map(
        functools.partial(on_device, sizes),
        mesh=mesh,
        in_specs=(rows, rows, rows, rows, rows, P("head"), P("head"), P("head"), P("head", None), P()),
        out_specs=P(("seq", "head"), None),
        check_vma=False,
    )
```

time: 212 us -> 94.2 us (0.44)
  Pallas kernels: 0 us -> 88.1 us
  blocking collectives: 60.8 us -> 0 us
  waiting for transfers between devices: 55.5 us -> 0 us
  matrix products: 32.8 us -> 0 us
  other arithmetic: 24.1 us -> 1.52 us
  local copies, waits for them, and re-layouts: 24.1 us -> 4.29 us
  between operations: 13.6 us -> 0.01 us
    pallas_call x0 -> x1, Pallas kernels: none -> 88.1 us  [on_device(): pl.pallas_call(functools.partial(layer_kernel, sizes), out_shape=jax.Shap...]
    all_gather x6 -> x0, blocking collectives: 52.3 us -> none  [the longest x4 33.4 us: entering(): lax.all_gather(part.astype(kind), axis)]
    reduce_scatter x1 -> x0, waiting for transfers between devices: 48.8 us -> none  [on_device(): lax.psum_scatter(jnp.dot(normed, w_out, preferred_element_type=jnp.float3...]
    dot_general x6 -> x0, matrix products: 32.8 us -> none  [the longest x1 10.7 us: on_device(): jnp.dot(normed, w_out, preferred_element_type=jnp.float32)]
    reshape x4 -> x0, local copies, waits for them, and re-layouts: 13.7 us -> none  [the longest x1 5.51 us: on_device(): y_total.reshape(rows_here, local_width)]
    another operation x11 -> x0, other arithmetic: 9.28 us -> none
    psum x1 -> x0, blocking collectives: 8.49 us -> none  [on_device(): all_squares = lax.psum(square_sums, 'head')]
    convert_element_type x12 -> x0, other arithmetic: 7.89 us -> none  [the longest x4 4.06 us: entering(): part.astype(kind)]
  transfers between devices with their start and end apart: 3 -> 0, of which waited for: 2 -> 0; matrix products, arithmetic and copies ran while one was open for 15% -> 0% of each run, Pallas kernels for 0% -> 0%
where the time goes in v1:
time: 94.2 us; the launch traced here: 94 us
  Pallas kernels  88.1 us (94%)
  local copies, waits for them, and re-layouts  4.29 us (5%)
  other arithmetic  1.52 us (2%)
    pallas_call x1, Pallas kernels, on_device(): pl.pallas_call(functools.partial(layer_kernel, sizes), out_shape=jax.Shap...  88.1 us
    unnamed x2, local copies, waits for them, and re-layouts  4.29 us

profile of v1, /device:TPU:1, one launch (start us, length us, event | category | flops | bytes accessed | tf_op | source)
XLA Modules:
  0.0 94.0 jit_solution(1505820962024134032)
XLA Ops:
  0.0 1.5 %maximum_bitcast_fusion.bc_ref = bf16[64,1024]{1,0:T(8,128)(2,1)} fusion(bf16[1024,32]{0,1:T(8,128)(2,1)} %param.13, bf16[1024,32]{0,1:T(8,128)(2,1)} %param.12), kind=kLoop, calls=%fused_computation | loop fusion | flops 262144 | bytes 262144 | tf_op jit(solution)/shard_map/transpose | solution.py:428
  1.5 1.8 %copy.11.dt_ref = f32[1024,16]{1,0:T(8,128)} copy(f32[1024,16]{0,1:T(8,128)} %param.14) | data formatting | bytes 131072 | tf_op args[4]
  3.4 88.1 %ssd_layer.1 = bf16[256,2560]{1,0:T(8,128)(2,1)} custom-call(bf16[64,1024]{1,0:T(8,128)(2,1)} %maximum_bitcast_fusion.bc_ref, f32[1024,16]{1,0:T(8,128)} %copy.11.dt_ref, f32[1,16]{1,0:T(1,128)} %bitcast.7, f32[1,16]{1,0:T(1,128)} %bitcast.8, f32[1,1024]{1,0:T(1,128)} %bitcast.6, s32[1,32]{1,0:T(1,128)} %bitcast.9, bf16[1024,1024]{1,0:T(8,128)(2,1)} %x_hbm.1, ...), custom_call_target="tpu_custom_call" | custom-call | tf_op jit(solution)/shard_map/ssd_layer/pallas_call | solution.py:435
  91.5 2.5 %copy.13 = bf16[256,2560]{1,0:T(8,128)(2,1)} copy(bf16[256,2560]{1,0:T(8,128)(2,1)} %ssd_layer.1) | data formatting | bytes 2621440

commit v2 on v1

--- a/solution.py
+++ b/solution.py
@@ -12,6 +12,27 @@
 MESH = pl.DeviceIdType.MESH
 F32 = jnp.float32
 BF16 = jnp.bfloat16
+
+
+CYCLES = (
+    (0, 1, 9, 8, 16, 24, 25, 17, 18, 10, 2, 26, 27, 3, 11, 19, 20, 28, 4, 12, 13, 21, 29, 5, 6, 14, 15, 23, 22, 30, 31, 7),
+    (0, 8, 15, 7, 6, 30, 29, 28, 27, 19, 18, 26, 25, 1, 2, 3, 4, 5, 13, 14, 22, 21, 20, 12, 11, 10, 9, 17, 16, 23, 31, 24),
+)
+CHIPS = len(CYCLES[0])
+HOPS = 14
+PLAN = (0, 1, 3, 2)
+
+
+def around(seq):
+    packed = 0
+    for chip in range(CHIPS):
+        for core in range(2):
+            cycle = CYCLES[core]
+            at = cycle.index(chip)
+            after, ahead = cycle[(at + 1) % CHIPS] * 2 + core, cycle[at - 1] * 2 + core
+            value = ((at * 64 + after) * 64 + ahead) * 32 + CYCLES[1 - core].index(chip)
+            packed = packed + jnp.where(seq == chip * 2 + core, value, 0)
+    return packed // 131072, packed // 2048 % 64, packed // 32 % 64, packed % 32
 
 
 def pieces(v, terms):
@@ -26,7 +47,7 @@
 def expand(v, spread, terms=2):
     total = None
     for part in pieces(v, terms):
-        term = jnp.dot(part, spread, preferred_element_type=F32)
+        term = lax.dot_general(part, spread, (((0,), (0,)), ((), ())), preferred_element_type=F32)
         total = term if total is None else total + term
     return total
 
@@ -37,20 +58,21 @@
 
 def layer_kernel(
     sizes,
-    bc_ref, dt_ref, rate_ref, skip_ref, gain_ref, docs_ref, x_hbm, z_hbm, w_hbm,
+    b_ref, c_ref, dt_ref, rate_ref, skip_ref, gain_ref, docs_ref, x_hbm, z_hbm, w_hbm,
     out_ref,
-    x_ref, z_ref, w_ref, bt_ref, ct_ref, xf_ref, e_ref, rows_ref, before_ref, ur_ref, as_ref,
+    x_ref, z_ref, wf_ref, bt_ref, ct_ref, xf_ref, e_ref, rows_ref, before_ref, ur_ref, as_ref,
     state_ref, decay_ref, got_state, got_decay, line_ref, got_line, back_ref, inc_ref, norm_ref,
-    sq_ref, got_sq, send_r, got_r, send_l, got_l,
+    sq_ref, got_sq, lhs_ref, relay_ref, acc_ref,
     in_sem, bc_send, bc_recv, st_send, st_recv, dc_send, dc_recv, ln_send, ln_recv, bk_send, bk_recv,
-    sq_send, sq_recv, r_send, r_recv, l_send, l_recv,
+    sq_send, sq_recv, y_send, y_recv, r_send, r_recv, l_send, l_recv, d_send, d_recv,
+    a_send, a_recv, f_send, f_recv,
 ):
     n_head, n_seq, line = sizes
     rows, width = x_ref.shape
-    heads = dt_ref.shape[1]
+    heads = dt_ref.shape[0]
     head_size = width // heads
     state_size = bt_ref.shape[0]
-    piece = bc_ref.shape[0] // 2
+    piece = b_ref.shape[0]
     spans = rows // SPAN
     me, seq = lax.axis_index("head"), lax.axis_index("seq")
     at_line, place = seq // line, seq % line
@@ -61,7 +83,7 @@
     def load(i, src, dst):
         return pltpu.make_async_copy(src, dst, in_sem.at[i])
 
-    loads = [load(0, x_hbm, x_ref), load(1, z_hbm, z_ref), load(2, w_hbm, w_ref)]
+    loads = [load(0, x_hbm, x_ref), load(1, z_hbm, z_ref), load(2, w_hbm, wf_ref.at[me])]
     for one in loads:
         one.start()
 
@@ -82,7 +104,7 @@
     def bc_copy(k, what, owner):
         dst = (bt_ref, ct_ref)[what].at[pl.ds(pl.multiple_of(owner * piece, piece), piece), :]
         return pltpu.make_async_remote_copy(
-            src_ref=bc_ref.at[pl.ds(what * piece, piece), :],
+            src_ref=(b_ref, c_ref)[what],
             dst_ref=dst,
             send_sem=bc_send.at[what, k],
             recv_sem=bc_recv.at[what, owner],
@@ -90,11 +112,112 @@
             device_id_type=MESH,
         )
 
+    core = seq % 2
+    partner = seq + 1 - 2 * core
+    spot, after, ahead_of, other_spot = around(seq // 2 * 2 + core)
+    out_width = wf_ref.shape[2]
+    slice_rows, side = wf_ref.shape[1] // CHIPS, out_width // 2
+
+    def shard(n):
+        return (me + (1, n_head - 1, 2)[n]) % n_head
+
+    def chunk(owner, position, column):
+        at = pl.multiple_of((position + CHIPS) % CHIPS * slice_rows, slice_rows)
+        return wf_ref.at[owner, pl.ds(at, slice_rows), pl.ds(pl.multiple_of(column * side, 128), side)]
+
+    def y_place(slot):
+        return spot if slot == 0 else spot + HOPS + slot
+
+    def y_copy(slot, k, owner):
+        where = chunk(owner, y_place(slot), core)
+        return pltpu.make_async_remote_copy(
+            src_ref=where,
+            dst_ref=where,
+            send_sem=y_send.at[slot, k],
+            recv_sem=y_recv.at[slot, owner],
+            device_id={"head": (me + k) % n_head},
+            device_id_type=MESH,
+        )
+
+    def right_copy(step, n, position):
+        where = chunk(shard(n), position, core)
+        return pltpu.make_async_remote_copy(
+            src_ref=where,
+            dst_ref=where,
+            send_sem=r_send.at[step, n],
+            recv_sem=r_recv.at[step, n],
+            device_id={"seq": after},
+            device_id_type=MESH,
+        )
+
+    def left_copy(step, n, position):
+        where = chunk(shard(n), position, core)
+        return pltpu.make_async_remote_copy(
+            src_ref=where,
+            dst_ref=where,
+            send_sem=l_send.at[step, n],
+            recv_sem=l_recv.at[step, n],
+            device_id={"seq": ahead_of},
+            device_id_type=MESH,
+        )
+
+    def partner_copy(e, n, position, column):
+        where = chunk(shard(n), position, column)
+        return pltpu.make_async_remote_copy(
+            src_ref=where,
+            dst_ref=where,
+            send_sem=d_send.at[e, n],
+            recv_sem=d_recv.at[e, n],
+            device_id={"seq": partner},
+            device_id_type=MESH,
+        )
+
+    def tick(u):
+        for n in range(n_head - 1):
+            step = u - n
+
+            @pl.when(step == 0)
+            def _():
+                y_copy(0, 1, shard(n)).wait_recv()
+                right_copy(0, n, spot).start()
+                left_copy(0, n, spot).start()
+                partner_copy(0, n, spot, core).start()
+
+            @pl.when((step >= 1) & (step <= HOPS))
+            def _():
+                right_copy(step - 1, n, spot - step).wait_recv()
+
+                @pl.when(step < HOPS)
+                def _():
+                    right_copy(step, n, spot - step).start()
+
+                partner_copy(step, n, spot - step, core).start()
+                left_copy(step - 1, n, spot + step).wait_recv()
+
+                @pl.when(step < HOPS)
+                def _():
+                    left_copy(step, n, spot + step).start()
+
+                partner_copy(HOPS + step, n, spot + step, core).start()
+
+    def ticks(first_tick, last_tick):
+        @pl.loop(first_tick, last_tick)
+        def _(u):
+            tick(u)
+
+    loads[2].wait()
     for what in range(2):
         for k in range(1, n_head):
             bc_copy(k, what, me).start()
+        for k in (n_head - 1, 1, 2):
+            if what == 0:
+                y_copy(0, k, me).start()
         mine = pl.ds(pl.multiple_of(me * piece, piece), piece)
-        (bt_ref, ct_ref)[what][mine, :] = bc_ref[what * piece : (what + 1) * piece, :]
+        (bt_ref, ct_ref)[what][mine, :] = (b_ref, c_ref)[what][...]
+
+    for slot in range(1, 4):
+        for k in range(1, n_head):
+            y_copy(slot, k, me).start()
 
     n_docs = docs_ref.shape[1]
     lengths = jnp.broadcast_to(docs_ref[...].astype(F32), (n_docs, n_docs))
@@ -120,34 +243,34 @@
         return col, row, previous, last
 
     spread = (iota((heads, width), 1) // head_size == iota((heads, width), 0)).astype(BF16)
-    below = (iota((SPAN, SPAN), 0) >= iota((SPAN, SPAN), 1)).astype(BF16)
+    own_lane = iota((heads, heads), 0) == iota((heads, heads), 1)
+    rate = jnp.sum(jnp.where(own_lane, rate_ref[...], 0.0), axis=1, keepdims=True)
+    skip = jnp.sum(jnp.where(own_lane, skip_ref[...], 0.0), axis=1, keepdims=True)
+    upto = (iota((SPAN, SPAN), 0) <= iota((SPAN, SPAN), 1)).astype(BF16)
 
     loads[0].wait()
 
     def scale_span(s, device_decay):
         at = pl.ds(pl.multiple_of(s * SPAN, SPAN), SPAN)
-        raw = dt_ref[at, :]
+        raw = dt_ref[:, at]
         step = jnp.maximum(raw, 0.0) + jnp.log(1.0 + jnp.exp(-jnp.abs(raw)))
         cum = None
-        for term in pieces(-step * rate_ref[...], 3):
-            sums = jnp.dot(below, term, preferred_element_type=F32)
+        for term in pieces(-step * rate, 3):
+            sums = jnp.dot(term, upto, preferred_element_type=F32)
             cum = sums if cum is None else cum + sums
-        middle = 0.5 * cum[SPAN - 1 : SPAN, :]
-        e_ref[at, :] = jnp.exp(cum - middle)
+        middle = 0.5 * cum[:, SPAN - 1 :]
+        e_ref[:, at] = jnp.exp(cum - middle)
         forward = step * jnp.exp(middle - cum)
         xf_ref[at, :] = (x_ref[at, :].astype(F32) * expand(forward, spread)).astype(BF16)
         _, _, previous, last = ids_of(s)
-        to_middle = jnp.exp(middle)
         total = jnp.exp(2.0 * middle) * jnp.where(last == previous, 1.0, 0.0)
-        both = jnp.concatenate(
-            [jnp.broadcast_to(to_middle, (8, heads)), jnp.broadcast_to(total, (8, heads))], axis=0
-        )
+        both = jnp.where(iota((heads, 16), 1) < 8, jnp.exp(middle), total)
         rows_ref[pl.ds(pl.multiple_of(s * 16, 16), 16), :] = expand(both, spread, 3)
         return device_decay * total
 
-    device_decay = lax.fori_loop(0, spans, scale_span, jnp.ones((1, heads), F32))
+    device_decay = lax.fori_loop(0, spans, scale_span, jnp.ones((heads, 1), F32))
     decay_ref[...] = jnp.zeros_like(decay_ref)
-    decay_ref[:, :heads] = jnp.broadcast_to(device_decay, (8, heads))
+    decay_ref[:, :heads] = jnp.broadcast_to(device_decay, (heads, 128)).T[:8, :]
 
     def line_peer(k):
         return {"seq": first + (place + k) % line}
@@ -212,10 +335,14 @@
     for k in range(1, n_head):
         bc_copy(k, 1, (me + n_head - k) % n_head).wait_recv()
     loads[1].wait()
-    skip_row = expand(jnp.broadcast_to(skip_ref[...], (8, heads)), spread, 3)[:1, :]
+    skip_row = expand(jnp.broadcast_to(skip, (heads, 8)), spread, 3)[:1, :]
+
+    ticks(0, PLAN[0])
 
     @pl.loop(0, spans)
     def _(s):
+        for i in range(PLAN[1]):
+            tick(PLAN[0] + s * PLAN[1] + i)
         at = pl.ds(pl.multiple_of(s * SPAN, SPAN), SPAN)
         col, row, previous, _ = ids_of(s)
         c_here = ct_ref[:, at].T
@@ -225,7 +352,7 @@
         local = jnp.dot(scores, xf_ref[at, :], preferred_element_type=F32)
         inter = jnp.dot(c_here, before_ref[s].astype(BF16), preferred_element_type=F32)
         base = pl.multiple_of(s * 16, 16)
-        out_of_middle = expand(e_ref[at, :], spread)
+        out_of_middle = expand(e_ref[:, at], spread)
         from_start = rows_ref[pl.ds(base, 1), :] * jnp.where(col == previous, 1.0, 0.0)
         gate = z_ref[at, :].astype(F32)
         gate = gate / (1.0 + jnp.exp(-gate))
@@ -243,7 +370,7 @@
 
     lanes = iota((128, half), 1) + (place % 2) * half
     spread_here = (lanes // head_size == iota((128, half), 0)).astype(BF16)
-    decays = expand(got_decay[...].reshape(line * 8, 128), spread_here, 3)
+    decays = expand(got_decay[...].reshape(line * 8, 128).T, spread_here, 3)
     inside, inc = [], jnp.zeros((part, half), F32)
     for d in range(line):
         inside.append(inc)
@@ -281,7 +408,9 @@
 
     inc_ref[own_part(place)] = back_ref[place]
 
-    loads[2].wait()
+    done = PLAN[0] + spans * PLAN[1]
+    ticks(done, done + PLAN[2])
+    done += PLAN[2]
 
     @pl.loop(1, line)
     def _(k):
@@ -314,69 +443,77 @@
             device_id_type=MESH,
         )
 
-    out_width = out_ref.shape[1]
-    parts, cut = got_r.shape[1], got_r.shape[3]
-
-    def product(block, column):
-        return jnp.dot(
-            norm_ref[pl.ds(pl.multiple_of(block * SPAN, SPAN), SPAN), :],
-            w_ref[:, pl.ds(pl.multiple_of(column, cut), cut)],
-            preferred_element_type=F32,
-        )
-
-    def right_copy(step, j):
-        return pltpu.make_async_remote_copy(
-            src_ref=send_r.at[step, j],
-            dst_ref=got_r.at[step, j],
-            send_sem=r_send.at[step, j],
-            recv_sem=r_recv.at[step, j],
-            device_id={"head": (me + 1) % n_head},
-            device_id_type=MESH,
-        )
-
-    def left_copy(step, j):
-        return pltpu.make_async_remote_copy(
-            src_ref=send_l.at[step, j],
-            dst_ref=got_l.at[step, j],
-            send_sem=l_send.at[step, j],
-            recv_sem=l_recv.at[step, j],
-            device_id={"head": (me + n_head - 1) % n_head},
-            device_id_type=MESH,
-        )
-
-    ahead, behind = (me + n_head - 1) % n_head, (me + 1) % n_head
-    finish(ahead)
-
-    @pl.loop(0, parts)
+    def rows_of(block, start=0, count=SPAN):
+        return norm_ref.at[pl.ds(pl.multiple_of(block * SPAN + start, count), count), :]
+
+    def block_copy(k, owner):
+        return pltpu.make_async_remote_copy(
+            src_ref=rows_of((me + k) % n_head),
+            dst_ref=lhs_ref.at[owner],
+            send_sem=a_send.at[k],
+            recv_sem=a_recv.at[owner],
+            device_id={"head": (me + k) % n_head},
+            device_id_type=MESH,
+        )
+
+    low = SPAN // 2
+    right, left, across_y = (me + 1) % n_head, (me + n_head - 1) % n_head, (me + 2) % n_head
+
+    def relay_copy(way):
+        return pltpu.make_async_remote_copy(
+            src_ref=rows_of(across_y, way * low, low),
+            dst_ref=relay_ref.at[way],
+            send_sem=f_send.at[way],
+            recv_sem=f_recv.at[way],
+            device_id={"head": (right, left)[way]},
+            device_id_type=MESH,
+        )
+
+    def forward_copy(way, owner):
+        return pltpu.make_async_remote_copy(
+            src_ref=relay_ref.at[way],
+            dst_ref=lhs_ref.at[owner, pl.ds(way * low, low), :],
+            send_sem=f_send.at[2 + way],
+            recv_sem=f_recv.at[2 + way],
+            device_id={"head": (right, left)[way]},
+            device_id_type=MESH,
+        )
+
+    finish(across_y)
+    square_copy(2, me).start()
+    relay_copy(0).start()
+    relay_copy(1).start()
+    finish(right)
+    square_copy(1, me).start()
+    block_copy(1, me).start()
+    finish(left)
+    square_copy(n_head - 1, me).start()
+    block_copy(n_head - 1, me).start()
+    finish(me)
+    ticks(done, done + PLAN[3])
+    done += PLAN[3]
+    relay_copy(0).wait_recv()
+    forward_copy(0, left).start()
+    relay_copy(1).wait_recv()
+    forward_copy(1, right).start()
+    ticks(done, HOPS + n_head - 1)
+
+    for slot in range(1, 4):
+        for n in range(n_head - 1):
+            y_copy(slot, 1, shard(n)).wait_recv()
+            partner_copy(2 * HOPS + slot, n, spot + HOPS + slot, core).start()
+
+    cut = 512
+
+    def product(lhs, owner, column):
+        return jnp.dot(lhs, wf_ref[owner, :, pl.ds(pl.multiple_of(column, cut), cut)], preferred_element_type=F32)
+
+    def columns(j):
+        return pl.ds(pl.multiple_of(j * cut, cut), cut)
+
+    @pl.loop(0, out_width // cut)
     def _(j):
-        send_r[0, j] = product(ahead, j * cut).astype(BF16)
-        right_copy(0, j).start()
-
-    finish(behind)
-
-    @pl.loop(0, parts)
-    def _(j):
-        send_l[0, j] = product(behind, out_width // 2 + j * cut).astype(BF16)
-        left_copy(0, j).start()
-
-    for k in range(2, n_head):
-        finish((me + k) % n_head) if k < n_head - 1 else finish(me)
-    for k in range(1, n_head):
-        square_copy(k, me).start()
-
-    for step in range(1, n_head - 1):
-        block_r, block_l = (me + 2 * n_head - 1 - step) % n_head, (me + 1 + step) % n_head
-
-        @pl.loop(0, parts)
-        def _(j):
-            own = product(block_r, j * cut)
-            right_copy(step - 1, j).wait_recv()
-            send_r[step, j] = (own + got_r[step - 1, j].astype(F32)).astype(BF16)
-            right_copy(step, j).start()
-            own = product(block_l, out_width // 2 + j * cut)
-            left_copy(step - 1, j).wait_recv()
-            send_l[step, j] = (own + got_l[step - 1, j].astype(F32)).astype(BF16)
-            left_copy(step, j).start()
+        acc_ref[:, columns(j)] = product(rows_of(me)[...], me, j * cut)
 
     total = sq_ref[me]
     for k in range(1, n_head):
@@ -385,18 +522,28 @@
         total = total + got_sq[owner]
     inverse_rms = lax.rsqrt(total / (width * n_head) + NORM_EPS).T[:, :1]
 
-    @pl.loop(0, parts)
+    def arrived(n):
+        @pl.loop(0, CHIPS)
+        def _(e):
+            place_of = jnp.where(e <= HOPS, other_spot - e, other_spot + e - HOPS)
+            partner_copy(e, n, place_of, 1 - core).wait_recv()
+
+    for n in range(2):
+        arrived(n)
+        block_copy((1, n_head - 1)[n], shard(n)).wait_recv()
+
+        @pl.loop(0, out_width // cut)
+        def _(j):
+            acc_ref[:, columns(j)] += product(lhs_ref[shard(n)], shard(n), j * cut)
+
+    arrived(2)
+    forward_copy(0, across_y).wait_recv()
+    forward_copy(1, across_y).wait_recv()
+
+    @pl.loop(0, out_width // cut)
     def _(j):
-        last = n_head - 2
-        own = product(me, j * cut)
-        right_copy(last, j).wait_recv()
-        own = (own + got_r[last, j].astype(F32)) * inverse_rms
-        out_ref[:, pl.ds(pl.multiple_of(j * cut, cut), cut)] = own.astype(BF16)
-        column = out_width // 2 + j * cut
-        own = product(me, column)
-        left_copy(last, j).wait_recv()
-        own = (own + got_l[last, j].astype(F32)) * inverse_rms
-        out_ref[:, pl.ds(pl.multiple_of(column, cut), cut)] = own.astype(BF16)
+        own = acc_ref[:, columns(j)] + product(lhs_ref[across_y], across_y, j * cut)
+        out_ref[:, columns(j)] = (own * inverse_rms).astype(BF16)
 
     for k in range(1, n_head):
         for what in range(2):
@@ -410,12 +557,25 @@
         back_copy(k, place).wait_send()
 
     line_copy.wait_send()
-    for step in range(n_head - 1):
-
-        @pl.loop(0, parts)
-        def _(j):
-            right_copy(step, j).wait_send()
-            left_copy(step, j).wait_send()
+    for slot in range(4):
+        for k in range(1, n_head):
+            y_copy(slot, k, me).wait_send()
+    for way in range(2):
+        relay_copy(way).wait_send()
+        forward_copy(way, across_y).wait_send()
+    block_copy(1, me).wait_send()
+    block_copy(n_head - 1, me).wait_send()
+
+    @pl.loop(0, HOPS)
+    def _(step):
+        for n in range(n_head - 1):
+            right_copy(step, n, spot - step).wait_send()
+            left_copy(step, n, spot + step).wait_send()
+
+    @pl.loop(0, CHIPS)
+    def _(e):
+        for n in range(n_head - 1):
+            partner_copy(e, n, spot + e, core).wait_send()
 
 
 def on_device(sizes, x_in, z_gate, b_in, c_in, dt_raw, decay_rate, skip_gain, norm_gain, w_out, doc_lengths):
@@ -425,26 +585,22 @@
     out_width = w_out.shape[1]
     state_size = b_in.shape[1] * n_head
     spans = rows // SPAN
-    bc = jnp.concatenate([b_in, c_in], axis=1).T
     part, half = state_size * 2 // line, width // 2
-    parts = 5
-    cut = out_width // 2 // parts
-    ring = (n_head - 1, parts, rows // n_head, cut)
     vmem, anywhere = pl.BlockSpec(memory_space=pltpu.VMEM), pl.BlockSpec(memory_space=pl.ANY)
     dma = pltpu.SemaphoreType.DMA
     return pl.pallas_call(
         functools.partial(layer_kernel, sizes),
         out_shape=jax.ShapeDtypeStruct((rows // n_head, out_width), BF16),
-        in_specs=[vmem] * 6 + [anywhere] * 3,
+        in_specs=[vmem] * 7 + [anywhere] * 3,
         out_specs=vmem,
         scratch_shapes=[
             pltpu.VMEM((rows, width), BF16),
             pltpu.VMEM((rows, width), BF16),
-            pltpu.VMEM(w_out.shape, BF16),
+            pltpu.VMEM((n_head, *w_out.shape), BF16),
             pltpu.VMEM((state_size, rows), BF16),
             pltpu.VMEM((state_size, rows), BF16),
             pltpu.VMEM((rows, width), BF16),
-            pltpu.VMEM((rows, heads), F32),
+            pltpu.VMEM((heads, rows), F32),
             pltpu.VMEM((spans * 16, width), F32),
             pltpu.VMEM((spans, state_size, width), F32),
             pltpu.VMEM((rows, width), F32),
@@ -460,10 +616,9 @@
             pltpu.VMEM((rows, width), BF16),
             pltpu.VMEM((n_head, 8, SPAN), F32),
             pltpu.VMEM((n_head, 8, SPAN), F32),
-            pltpu.VMEM(ring, BF16),
-            pltpu.VMEM(ring, BF16),
-            pltpu.VMEM(ring, BF16),
-            pltpu.VMEM(ring, BF16),
+            pltpu.VMEM((n_head, rows // n_head, width), BF16),
+            pltpu.VMEM((2, rows // n_head // 2, width), BF16),
+            pltpu.VMEM((rows // n_head, out_width), F32),
             dma((3,)),
             dma((2, n_head)),
             dma((2, n_head)),
@@ -477,18 +632,27 @@
             dma((line,)),
             dma((n_head,)),
             dma((n_head,)),
-            dma((n_head - 1, parts)),
-            dma((n_head - 1, parts)),
-            dma((n_head - 1, parts)),
-            dma((n_head - 1, parts)),
+            dma((4, n_head)),
+            dma((4, n_head)),
+            dma((HOPS, n_head - 1)),
+            dma((HOPS, n_head - 1)),
+            dma((HOPS, n_head - 1)),
+            dma((HOPS, n_head - 1)),
+            dma((CHIPS, n_head - 1)),
+            dma((CHIPS, n_head - 1)),
+            dma((n_head,)),
+            dma((n_head,)),
+            dma((4,)),
+            dma((4,)),
         ],
         compiler_params=pltpu.CompilerParams(
             collective_id=0, has_side_effects=True, vmem_limit_bytes=60 * 1024 * 1024
         ),
         name="ssd_layer",
     )(
-        bc,
-        dt_raw,
+        b_in.T,
+        c_in.T,
+        dt_raw.T,
         decay_rate[None, :],
         skip_gain[None, :],
         norm_gain[None, :],

time: 94.2 us -> 113 us (1.20)
  Pallas kernels: 88.1 us -> 111 us
  local copies, waits for them, and re-layouts: 4.29 us -> 2.46 us
  other arithmetic: 1.52 us -> 0 us
    pallas_call x1, Pallas kernels: 88.1 us -> 111 us  [on_device(): pl.pallas_call(functools.partial(layer_kernel, sizes), out_shape=jax.Shap...]
    unnamed x2 -> x1, local copies, waits for them, and re-layouts: 4.29 us -> 2.46 us
    transpose x1 -> x0, other arithmetic: 1.52 us -> none  [on_device(): bc = jnp.concatenate([b_in, c_in], axis=1).T]
where the time goes in v2:
time: 113 us
  Pallas kernels  111 us (98%)
  local copies, waits for them, and re-layouts  2.46 us (2%)
    pallas_call x1, Pallas kernels, on_device(): pl.pallas_call(functools.partial(layer_kernel, sizes), out_shape=jax.Shap...  111 us
    unnamed x1, local copies, waits for them, and re-layouts  2.46 us

profile of v2, /device:TPU:1, one launch (start us, length us, event | category | flops | bytes accessed | tf_op | source)
XLA Modules:
  0.0 113.3 jit_solution(2899743890201302966)
XLA Ops:
  0.0 110.8 %ssd_layer.1 = bf16[256,2560]{1,0:T(8,128)(2,1)} custom-call(bf16[32,1024]{1,0:T(8,128)(2,1)} %bitcast.7, bf16[32,1024]{1,0:T(8,128)(2,1)} %bitcast.8, f32[16,1024]{1,0:T(8,128)} %bitcast.9, f32[1,16]{1,0:T(1,128)} %bitcast.11, f32[1,16]{1,0:T(1,128)} %bitcast.12, f32[1,1024]{1,0:T(1,128)} %bitcast.10, s32[1,32]{1,0:T(1,128)} %bitcast.13, ...), custom_call_target="tpu_custom_call" | custom-call | tf_op jit(solution)/shard_map/ssd_layer/pallas_call | solution.py:591
  110.8 2.5 %copy.12 = bf16[256,2560]{1,0:T(8,128)(2,1)} copy(bf16[256,2560]{1,0:T(8,128)(2,1)} %ssd_layer.1) | data formatting | bytes 2621440

commit v3 on v2

--- a/solution.py
+++ b/solution.py
@@ -14,25 +14,43 @@
 BF16 = jnp.bfloat16
 
 
-CYCLES = (
-    (0, 1, 9, 8, 16, 24, 25, 17, 18, 10, 2, 26, 27, 3, 11, 19, 20, 28, 4, 12, 13, 21, 29, 5, 6, 14, 15, 23, 22, 30, 31, 7),
-    (0, 8, 15, 7, 6, 30, 29, 28, 27, 19, 18, 26, 25, 1, 2, 3, 4, 5, 13, 14, 22, 21, 20, 12, 11, 10, 9, 17, 16, 23, 31, 24),
-)
-CHIPS = len(CYCLES[0])
-HOPS = 14
-PLAN = (0, 1, 3, 2)
-
-
-def around(seq):
-    packed = 0
-    for chip in range(CHIPS):
-        for core in range(2):
-            cycle = CYCLES[core]
-            at = cycle.index(chip)
-            after, ahead = cycle[(at + 1) % CHIPS] * 2 + core, cycle[at - 1] * 2 + core
-            value = ((at * 64 + after) * 64 + ahead) * 32 + CYCLES[1 - core].index(chip)
-            packed = packed + jnp.where(seq == chip * 2 + core, value, 0)
-    return packed // 131072, packed // 2048 % 64, packed // 32 % 64, packed % 32
+SIDES = (1792, 768)
+PLAN = (3, 6, 4)
+PLANE = (8, 4)
+CHIPS = PLANE[0] * PLANE[1]
+
+
+def gather_steps(core):
+    one, two = (0, 1) if core == 0 else (1, 0)
+
+    def moved(by_one, by_two):
+        return (by_one, by_two) if core == 0 else (by_two, by_one)
+
+    def hops(axis, opposite):
+        size = PLANE[axis]
+        rows = []
+        for hop in range(1, size // 2 + 1):
+            row = []
+            for way in range(2):
+                if hop < size // 2 or way == opposite:
+                    goes_on = hop + 1 < size // 2 or (hop + 1 == size // 2 and way == opposite)
+                    row.append((hop if way else -hop, 2 * axis + way, goes_on))
+            rows.append(row)
+        return rows
+
+    both = [2 * two, 2 * two + 1]
+    first = hops(one, 0)
+    lines = [(0, 0)] + [(offset, hop + 1) for hop, row in enumerate(first) for offset, _, _ in row]
+    steps = []
+    for when in range(1, PLANE[one] // 2 + PLANE[two] // 2 + 1):
+        if when <= len(first):
+            for offset, way, goes_on in first[when - 1]:
+                steps.append((*moved(offset, 0), both + ([way] if goes_on else [])))
+        for i, (line_offset, ready) in enumerate(lines):
+            if 1 <= when - ready <= PLANE[two] // 2:
+                for offset, way, goes_on in hops(two, i % 2)[when - ready - 1]:
+                    steps.append((*moved(line_offset, offset), [way] if goes_on else []))
+    return steps
 
 
 def pieces(v, terms):
@@ -64,7 +82,7 @@
     state_ref, decay_ref, got_state, got_decay, line_ref, got_line, back_ref, inc_ref, norm_ref,
     sq_ref, got_sq, lhs_ref, relay_ref, acc_ref,
     in_sem, bc_send, bc_recv, st_send, st_recv, dc_send, dc_recv, ln_send, ln_recv, bk_send, bk_recv,
-    sq_send, sq_recv, y_send, y_recv, r_send, r_recv, l_send, l_recv, d_send, d_recv,
+    sq_send, sq_recv, y_send, y_recv, w_send, w_recv, d_send, d_recv,
     a_send, a_recv, f_send, f_recv,
 ):
     n_head, n_seq, line = sizes
@@ -83,7 +101,7 @@
     def load(i, src, dst):
         return pltpu.make_async_copy(src, dst, in_sem.at[i])
 
-    loads = [load(0, x_hbm, x_ref), load(1, z_hbm, z_ref), load(2, w_hbm, wf_ref.at[me])]
+    loads = [load(0, x_hbm, x_ref), load(1, z_hbm, z_ref), load(2, w_hbm, wf_ref.at[n_head - 1])]
     for one in loads:
         one.start()
 
@@ -114,110 +132,93 @@
 
     core = seq % 2
     partner = seq + 1 - 2 * core
-    spot, after, ahead_of, other_spot = around(seq // 2 * 2 + core)
     out_width = wf_ref.shape[2]
-    slice_rows, side = wf_ref.shape[1] // CHIPS, out_width // 2
+    slice_rows = wf_ref.shape[1] // CHIPS
+    mine_of_w = n_head - 1
+    ways = (
+        first + (place + 2) % line,
+        first + (place + line - 2) % line,
+        (seq + line) % n_seq,
+        (seq + n_seq - line) % n_seq,
+    )
+
+    def chip(along_z, along_x):
+        return (at_line + along_x + PLANE[1]) % PLANE[1] * PLANE[0] + (place // 2 + along_z + PLANE[0]) % PLANE[0]
 
     def shard(n):
         return (me + (1, n_head - 1, 2)[n]) % n_head
 
-    def chunk(owner, position, column):
-        at = pl.multiple_of((position + CHIPS) % CHIPS * slice_rows, slice_rows)
-        return wf_ref.at[owner, pl.ds(at, slice_rows), pl.ds(pl.multiple_of(column * side, 128), side)]
-
-    def y_place(slot):
-        return spot if slot == 0 else spot + HOPS + slot
-
-    def y_copy(slot, k, owner):
-        where = chunk(owner, y_place(slot), core)
+    def chunk(of_core, index, who):
+        at = pl.multiple_of(who * slice_rows, slice_rows)
+        side = pl.ds(0 if of_core == 0 else SIDES[0], SIDES[of_core])
+        return wf_ref.at[index, pl.ds(at, slice_rows), side]
+
+    def y_copy(of_core, k, index):
+        return pltpu.make_async_remote_copy(
+            src_ref=chunk(of_core, mine_of_w, chip(0, 0)),
+            dst_ref=chunk(of_core, index, chip(0, 0)),
+            send_sem=y_send.at[k],
+            recv_sem=y_recv.at[index],
+            device_id={"head": (me + k) % n_head},
+            device_id_type=MESH,
+        )
+
+    def slice_copy(of_core, who, way):
+        where = chunk(of_core, pl.ds(0, n_head - 1), who)
         return pltpu.make_async_remote_copy(
             src_ref=where,
             dst_ref=where,
-            send_sem=y_send.at[slot, k],
-            recv_sem=y_recv.at[slot, owner],
-            device_id={"head": (me + k) % n_head},
-            device_id_type=MESH,
-        )
-
-    def right_copy(step, n, position):
-        where = chunk(shard(n), position, core)
+            send_sem=w_send.at[way, who],
+            recv_sem=w_recv.at[who],
+            device_id={"seq": ways[way]},
+            device_id_type=MESH,
+        )
+
+    def partner_copy(of_core, who):
+        where = chunk(of_core, pl.ds(0, n_head - 1), who)
         return pltpu.make_async_remote_copy(
             src_ref=where,
             dst_ref=where,
-            send_sem=r_send.at[step, n],
-            recv_sem=r_recv.at[step, n],
-            device_id={"seq": after},
-            device_id_type=MESH,
-        )
-
-    def left_copy(step, n, position):
-        where = chunk(shard(n), position, core)
-        return pltpu.make_async_remote_copy(
-            src_ref=where,
-            dst_ref=where,
-            send_sem=l_send.at[step, n],
-            recv_sem=l_recv.at[step, n],
-            device_id={"seq": ahead_of},
-            device_id_type=MESH,
-        )
-
-    def partner_copy(e, n, position, column):
-        where = chunk(shard(n), position, column)
-        return pltpu.make_async_remote_copy(
-            src_ref=where,
-            dst_ref=where,
-            send_sem=d_send.at[e, n],
-            recv_sem=d_recv.at[e, n],
+            send_sem=d_send.at[who],
+            recv_sem=d_recv.at[who],
             device_id={"seq": partner},
             device_id_type=MESH,
         )
 
-    def tick(u):
+    def on_each_core(what):
+        for of_core in range(2):
+            pl.when(core == of_core)(functools.partial(what, of_core))
+
+    def start_gather(of_core):
         for n in range(n_head - 1):
-            step = u - n
-
-            @pl.when(step == 0)
-            def _():
-                y_copy(0, 1, shard(n)).wait_recv()
-                right_copy(0, n, spot).start()
-                left_copy(0, n, spot).start()
-                partner_copy(0, n, spot, core).start()
-
-            @pl.when((step >= 1) & (step <= HOPS))
-            def _():
-                right_copy(step - 1, n, spot - step).wait_recv()
-
-                @pl.when(step < HOPS)
-                def _():
-                    right_copy(step, n, spot - step).start()
-
-                partner_copy(step, n, spot - step, core).start()
-                left_copy(step - 1, n, spot + step).wait_recv()
-
-                @pl.when(step < HOPS)
-                def _():
-                    left_copy(step, n, spot + step).start()
-
-                partner_copy(HOPS + step, n, spot + step, core).start()
-
-    def ticks(first_tick, last_tick):
-        @pl.loop(first_tick, last_tick)
-        def _(u):
-            tick(u)
+            y_copy(of_core, 1, n).wait_recv()
+        for way in range(4):
+            slice_copy(of_core, chip(0, 0), way).start()
+        partner_copy(of_core, chip(0, 0)).start()
+
+    def gather(first_step, last_step):
+        def run(of_core):
+            for along_z, along_x, on in gather_steps(of_core)[first_step:last_step]:
+                who = chip(along_z, along_x)
+                slice_copy(of_core, who, 0).wait_recv()
+                for way in on:
+                    slice_copy(of_core, who, way).start()
+                partner_copy(of_core, who).start()
+
+        on_each_core(run)
+
+    def start_y(of_core):
+        for k, index in ((1, 1), (n_head - 1, 0), (2, 2)):
+            y_copy(of_core, k, index).start()
 
     loads[2].wait()
     for what in range(2):
         for k in range(1, n_head):
             bc_copy(k, what, me).start()
-        for k in (n_head - 1, 1, 2):
-            if what == 0:
-                y_copy(0, k, me).start()
+        if what == 0:
+            on_each_core(start_y)
         mine = pl.ds(pl.multiple_of(me * piece, piece), piece)
         (bt_ref, ct_ref)[what][mine, :] = (b_ref, c_ref)[what][...]
-
-    for slot in range(1, 4):
-        for k in range(1, n_head):
-            y_copy(slot, k, me).start()
 
     n_docs = docs_ref.shape[1]
     lengths = jnp.broadcast_to(docs_ref[...].astype(F32), (n_docs, n_docs))
@@ -337,12 +338,10 @@
     loads[1].wait()
     skip_row = expand(jnp.broadcast_to(skip, (heads, 8)), spread, 3)[:1, :]
 
-    ticks(0, PLAN[0])
+    on_each_core(start_gather)
 
     @pl.loop(0, spans)
     def _(s):
-        for i in range(PLAN[1]):
-            tick(PLAN[0] + s * PLAN[1] + i)
         at = pl.ds(pl.multiple_of(s * SPAN, SPAN), SPAN)
         col, row, previous, _ = ids_of(s)
         c_here = ct_ref[:, at].T
@@ -359,6 +358,8 @@
         y = out_of_middle * (local + from_start * inter) + skip_row * x_ref[at, :].astype(F32)
         ur_ref[at, :] = y * gate
         as_ref[at, :] = out_of_middle * from_start * gate
+
+    gather(0, PLAN[0])
 
     @pl.loop(1, line)
     def _(k):
@@ -408,9 +409,7 @@
 
     inc_ref[own_part(place)] = back_ref[place]
 
-    done = PLAN[0] + spans * PLAN[1]
-    ticks(done, done + PLAN[2])
-    done += PLAN[2]
+    gather(PLAN[0], PLAN[0] + PLAN[1])
 
     @pl.loop(1, line)
     def _(k):
@@ -490,18 +489,12 @@
     square_copy(n_head - 1, me).start()
     block_copy(n_head - 1, me).start()
     finish(me)
-    ticks(done, done + PLAN[3])
-    done += PLAN[3]
+    gather(PLAN[0] + PLAN[1], sum(PLAN))
     relay_copy(0).wait_recv()
     forward_copy(0, left).start()
     relay_copy(1).wait_recv()
     forward_copy(1, right).start()
-    ticks(done, HOPS + n_head - 1)
-
-    for slot in range(1, 4):
-        for n in range(n_head - 1):
-            y_copy(slot, 1, shard(n)).wait_recv()
-            partner_copy(2 * HOPS + slot, n, spot + HOPS + slot, core).start()
+    gather(sum(PLAN), CHIPS)
 
     cut = 512
 
@@ -513,7 +506,7 @@
 
     @pl.loop(0, out_width // cut)
     def _(j):
-        acc_ref[:, columns(j)] = product(rows_of(me)[...], me, j * cut)
+        acc_ref[:, columns(j)] = product(rows_of(me)[...], mine_of_w, j * cut)
 
     total = sq_ref[me]
     for k in range(1, n_head):
@@ -522,27 +515,25 @@
         total = total + got_sq[owner]
     inverse_rms = lax.rsqrt(total / (width * n_head) + NORM_EPS).T[:, :1]
 
-    def arrived(n):
+    def other_half(of_core):
         @pl.loop(0, CHIPS)
-        def _(e):
-            place_of = jnp.where(e <= HOPS, other_spot - e, other_spot + e - HOPS)
-            partner_copy(e, n, place_of, 1 - core).wait_recv()
-
+        def _(who):
+            partner_copy(1 - of_core, who).wait_recv()
+
+    on_each_core(other_half)
     for n in range(2):
-        arrived(n)
         block_copy((1, n_head - 1)[n], shard(n)).wait_recv()
 
         @pl.loop(0, out_width // cut)
         def _(j):
-            acc_ref[:, columns(j)] += product(lhs_ref[shard(n)], shard(n), j * cut)
-
-    arrived(2)
+            acc_ref[:, columns(j)] += product(lhs_ref[shard(n)], n, j * cut)
+
     forward_copy(0, across_y).wait_recv()
     forward_copy(1, across_y).wait_recv()
 
     @pl.loop(0, out_width // cut)
     def _(j):
-        own = acc_ref[:, columns(j)] + product(lhs_ref[across_y], across_y, j * cut)
+        own = acc_ref[:, columns(j)] + product(lhs_ref[across_y], 2, j * cut)
         out_ref[:, columns(j)] = (own * inverse_rms).astype(BF16)
 
     for k in range(1, n_head):
@@ -557,25 +548,26 @@
         back_copy(k, place).wait_send()
 
     line_copy.wait_send()
-    for slot in range(4):
-        for k in range(1, n_head):
-            y_copy(slot, k, me).wait_send()
     for way in range(2):
         relay_copy(way).wait_send()
         forward_copy(way, across_y).wait_send()
     block_copy(1, me).wait_send()
     block_copy(n_head - 1, me).wait_send()
 
-    @pl.loop(0, HOPS)
-    def _(step):
-        for n in range(n_head - 1):
-            right_copy(step, n, spot - step).wait_send()
-            left_copy(step, n, spot + step).wait_send()
-
-    @pl.loop(0, CHIPS)
-    def _(e):
-        for n in range(n_head - 1):
-            partner_copy(e, n, spot + e, core).wait_send()
+    def all_left(of_core):
+        for k in range(1, n_head):
+            y_copy(of_core, k, 0).wait_send()
+        for way in range(4):
+            slice_copy(of_core, chip(0, 0), way).wait_send()
+        for along_z, along_x, on in gather_steps(of_core):
+            for way in on:
+                slice_copy(of_core, chip(along_z, along_x), way).wait_send()
+
+        @pl.loop(0, CHIPS)
+        def _(who):
+            partner_copy(of_core, who).wait_send()
+
+    on_each_core(all_left)
 
 
 def on_device(sizes, x_in, z_gate, b_in, c_in, dt_raw, decay_rate, skip_gain, norm_gain, w_out, doc_lengths):
@@ -632,14 +624,12 @@
             dma((line,)),
             dma((n_head,)),
             dma((n_head,)),
-            dma((4, n_head)),
-            dma((4, n_head)),
-            dma((HOPS, n_head - 1)),
-            dma((HOPS, n_head - 1)),
-            dma((HOPS, n_head - 1)),
-            dma((HOPS, n_head - 1)),
-            dma((CHIPS, n_head - 1)),
-            dma((CHIPS, n_head - 1)),
+            dma((n_head,)),
+            dma((n_head,)),
+            dma((4, CHIPS)),
+            dma((CHIPS,)),
+            dma((CHIPS,)),
+            dma((CHIPS,)),
             dma((n_head,)),
             dma((n_head,)),
             dma((4,)),

time: 113 us -> 104 us (0.920)
  Pallas kernels: 111 us -> 102 us
    pallas_call x1, Pallas kernels: 111 us -> 102 us  [on_device(): pl.pallas_call(functools.partial(layer_kernel, sizes), out_shape=jax.Shap...]
where the time goes in v3:
time: 104 us
  Pallas kernels  102 us (98%)
  local copies, waits for them, and re-layouts  2.46 us (2%)
    pallas_call x1, Pallas kernels, on_device(): pl.pallas_call(functools.partial(layer_kernel, sizes), out_shape=jax.Shap...  102 us
    unnamed x1, local copies, waits for them, and re-layouts  2.46 us

profile of v3, /device:TPU:1, one launch (start us, length us, event | category | flops | bytes accessed | tf_op | source)
XLA Modules:
  0.0 104.2 jit_solution(12004985048100455390)
XLA Ops:
  0.0 101.7 %ssd_layer.1 = bf16[256,2560]{1,0:T(8,128)(2,1)} custom-call(bf16[32,1024]{1,0:T(8,128)(2,1)} %bitcast.7, bf16[32,1024]{1,0:T(8,128)(2,1)} %bitcast.8, f32[16,1024]{1,0:T(8,128)} %bitcast.9, f32[1,16]{1,0:T(1,128)} %bitcast.11, f32[1,16]{1,0:T(1,128)} %bitcast.12, f32[1,1024]{1,0:T(1,128)} %bitcast.10, s32[1,32]{1,0:T(1,128)} %bitcast.13, ...), custom_call_target="tpu_custom_call" | custom-call | tf_op jit(solution)/shard_map/ssd_layer/pallas_call | solution.py:583
  101.7 2.5 %copy.12 = bf16[256,2560]{1,0:T(8,128)(2,1)} copy(bf16[256,2560]{1,0:T(8,128)(2,1)} %ssd_layer.1) | data formatting | bytes 2621440

commit v4 on v1

--- a/solution.py
+++ b/solution.py
@@ -26,7 +26,7 @@
 def expand(v, spread, terms=2):
     total = None
     for part in pieces(v, terms):
-        term = jnp.dot(part, spread, preferred_element_type=F32)
+        term = lax.dot_general(part, spread, (((0,), (0,)), ((), ())), preferred_element_type=F32)
         total = term if total is None else total + term
     return total
 
@@ -37,20 +37,20 @@
 
 def layer_kernel(
     sizes,
-    bc_ref, dt_ref, rate_ref, skip_ref, gain_ref, docs_ref, x_hbm, z_hbm, w_hbm,
+    b_hbm, c_hbm, dt_hbm, rate_hbm, skip_hbm, gain_hbm, docs_hbm, x_hbm, z_hbm, w_hbm,
     out_ref,
-    x_ref, z_ref, w_ref, bt_ref, ct_ref, xf_ref, e_ref, rows_ref, before_ref, ur_ref, as_ref,
+    b_ref, c_ref, dt_ref, rate_ref, skip_ref, gain_ref, docs_ref, x_ref, z_ref, w_ref, bt_ref, ct_ref, xf_ref, e_ref, rows_ref, before_ref, ur_ref, as_ref,
     state_ref, decay_ref, got_state, got_decay, line_ref, got_line, back_ref, inc_ref, norm_ref,
-    sq_ref, got_sq, send_r, got_r, send_l, got_l,
+    sq_ref, got_sq, send_r, got_r, send_l, got_l, decays_ref,
     in_sem, bc_send, bc_recv, st_send, st_recv, dc_send, dc_recv, ln_send, ln_recv, bk_send, bk_recv,
     sq_send, sq_recv, r_send, r_recv, l_send, l_recv,
 ):
     n_head, n_seq, line = sizes
     rows, width = x_ref.shape
-    heads = dt_ref.shape[1]
+    heads = dt_ref.shape[0]
     head_size = width // heads
     state_size = bt_ref.shape[0]
-    piece = bc_ref.shape[0] // 2
+    piece = b_ref.shape[0]
     spans = rows // SPAN
     me, seq = lax.axis_index("head"), lax.axis_index("seq")
     at_line, place = seq // line, seq % line
@@ -61,10 +61,6 @@
     def load(i, src, dst):
         return pltpu.make_async_copy(src, dst, in_sem.at[i])
 
-    loads = [load(0, x_hbm, x_ref), load(1, z_hbm, z_ref), load(2, w_hbm, w_ref)]
-    for one in loads:
-        one.start()
-
     barrier = pltpu.get_barrier_semaphore()
     for k in range(1, n_head):
         pl.semaphore_signal(barrier, inc=1, device_id={"head": (me + k) % n_head}, device_id_type=MESH)
@@ -77,12 +73,20 @@
 
     for step in (line, n_seq - line):
         pl.semaphore_signal(barrier, inc=1, device_id={"seq": (seq + step) % n_seq}, device_id_type=MESH)
+    sources = (b_hbm, dt_hbm, rate_hbm, docs_hbm, x_hbm, c_hbm, skip_hbm, gain_hbm, z_hbm, w_hbm)
+    targets = (b_ref, dt_ref, rate_ref, docs_ref, x_ref, c_ref, skip_ref, gain_ref, z_ref, w_ref)
+    loads = [load(i, *pair) for i, pair in enumerate(zip(sources, targets))]
+    for one in loads:
+        one.start()
+    for one in loads[:4]:
+        one.wait()
+    loads[5].wait()
     pl.semaphore_wait(barrier, n_head - 1 + line - 1 + 2)
 
     def bc_copy(k, what, owner):
         dst = (bt_ref, ct_ref)[what].at[pl.ds(pl.multiple_of(owner * piece, piece), piece), :]
         return pltpu.make_async_remote_copy(
-            src_ref=bc_ref.at[pl.ds(what * piece, piece), :],
+            src_ref=(b_ref, c_ref)[what],
             dst_ref=dst,
             send_sem=bc_send.at[what, k],
             recv_sem=bc_recv.at[what, owner],
@@ -94,7 +98,7 @@
         for k in range(1, n_head):
             bc_copy(k, what, me).start()
         mine = pl.ds(pl.multiple_of(me * piece, piece), piece)
-        (bt_ref, ct_ref)[what][mine, :] = bc_ref[what * piece : (what + 1) * piece, :]
+        (bt_ref, ct_ref)[what][mine, :] = (b_ref, c_ref)[what][...]
 
     n_docs = docs_ref.shape[1]
     lengths = jnp.broadcast_to(docs_ref[...].astype(F32), (n_docs, n_docs))
@@ -120,34 +124,33 @@
         return col, row, previous, last
 
     spread = (iota((heads, width), 1) // head_size == iota((heads, width), 0)).astype(BF16)
-    below = (iota((SPAN, SPAN), 0) >= iota((SPAN, SPAN), 1)).astype(BF16)
-
-    loads[0].wait()
+    own_lane = iota((heads, heads), 0) == iota((heads, heads), 1)
+    rate = jnp.sum(jnp.where(own_lane, rate_ref[...], 0.0), axis=1, keepdims=True)
+    upto = (iota((SPAN, SPAN), 0) <= iota((SPAN, SPAN), 1)).astype(BF16)
+
+    loads[4].wait()
 
     def scale_span(s, device_decay):
         at = pl.ds(pl.multiple_of(s * SPAN, SPAN), SPAN)
-        raw = dt_ref[at, :]
+        raw = dt_ref[:, at]
         step = jnp.maximum(raw, 0.0) + jnp.log(1.0 + jnp.exp(-jnp.abs(raw)))
         cum = None
-        for term in pieces(-step * rate_ref[...], 3):
-            sums = jnp.dot(below, term, preferred_element_type=F32)
+        for term in pieces(-step * rate, 3):
+            sums = jnp.dot(term, upto, preferred_element_type=F32)
             cum = sums if cum is None else cum + sums
-        middle = 0.5 * cum[SPAN - 1 : SPAN, :]
-        e_ref[at, :] = jnp.exp(cum - middle)
+        middle = 0.5 * cum[:, SPAN - 1 :]
+        e_ref[:, at] = jnp.exp(cum - middle)
         forward = step * jnp.exp(middle - cum)
         xf_ref[at, :] = (x_ref[at, :].astype(F32) * expand(forward, spread)).astype(BF16)
         _, _, previous, last = ids_of(s)
-        to_middle = jnp.exp(middle)
         total = jnp.exp(2.0 * middle) * jnp.where(last == previous, 1.0, 0.0)
-        both = jnp.concatenate(
-            [jnp.broadcast_to(to_middle, (8, heads)), jnp.broadcast_to(total, (8, heads))], axis=0
-        )
+        both = jnp.where(iota((heads, 16), 1) < 8, jnp.exp(middle), total)
         rows_ref[pl.ds(pl.multiple_of(s * 16, 16), 16), :] = expand(both, spread, 3)
         return device_decay * total
 
-    device_decay = lax.fori_loop(0, spans, scale_span, jnp.ones((1, heads), F32))
+    device_decay = lax.fori_loop(0, spans, scale_span, jnp.ones((heads, 1), F32))
     decay_ref[...] = jnp.zeros_like(decay_ref)
-    decay_ref[:, :heads] = jnp.broadcast_to(device_decay, (8, heads))
+    decay_ref[:, :heads] = jnp.broadcast_to(device_decay, (heads, 128)).T[:8, :]
 
     def line_peer(k):
         return {"seq": first + (place + k) % line}
@@ -209,10 +212,19 @@
 
     got_state[place] = state_ref[own_part(place)]
 
+    @pl.loop(1, line)
+    def _(k):
+        decay_copy(k, from_peer(k)).wait_recv()
+
+    lanes = iota((128, half), 1) + (place % 2) * half
+    spread_here = (lanes // head_size == iota((128, half), 0)).astype(BF16)
+    decays_ref[...] = expand(got_decay[...].reshape(line * 8, 128).T, spread_here, 3)
     for k in range(1, n_head):
         bc_copy(k, 1, (me + n_head - k) % n_head).wait_recv()
-    loads[1].wait()
-    skip_row = expand(jnp.broadcast_to(skip_ref[...], (8, heads)), spread, 3)[:1, :]
+    for one in loads[6:9]:
+        one.wait()
+    skip = jnp.sum(jnp.where(own_lane, skip_ref[...], 0.0), axis=1, keepdims=True)
+    skip_row = expand(jnp.broadcast_to(skip, (heads, 8)), spread, 3)[:1, :]
 
     @pl.loop(0, spans)
     def _(s):
@@ -225,7 +237,7 @@
         local = jnp.dot(scores, xf_ref[at, :], preferred_element_type=F32)
         inter = jnp.dot(c_here, before_ref[s].astype(BF16), preferred_element_type=F32)
         base = pl.multiple_of(s * 16, 16)
-        out_of_middle = expand(e_ref[at, :], spread)
+        out_of_middle = expand(e_ref[:, at], spread)
         from_start = rows_ref[pl.ds(base, 1), :] * jnp.where(col == previous, 1.0, 0.0)
         gate = z_ref[at, :].astype(F32)
         gate = gate / (1.0 + jnp.exp(-gate))
@@ -235,19 +247,12 @@
 
     @pl.loop(1, line)
     def _(k):
-        decay_copy(k, from_peer(k)).wait_recv()
-
-    @pl.loop(1, line)
-    def _(k):
         state_copy(k, from_peer(k)).wait_recv()
 
-    lanes = iota((128, half), 1) + (place % 2) * half
-    spread_here = (lanes // head_size == iota((128, half), 0)).astype(BF16)
-    decays = expand(got_decay[...].reshape(line * 8, 128), spread_here, 3)
     inside, inc = [], jnp.zeros((part, half), F32)
     for d in range(line):
         inside.append(inc)
-        inc = decays[8 * d : 8 * d + 1, :] * inc + got_state[d].astype(F32)
+        inc = decays_ref[8 * d : 8 * d + 1, :] * inc + got_state[d].astype(F32)
     line_ref[...] = inc
     line_copy = pltpu.make_async_remote_copy(
         src_ref=line_ref,
@@ -263,7 +268,7 @@
     earlier = got_line[...]
     for d in range(line):
         back_ref[d] = (inside[d] + factor * earlier).astype(BF16)
-        factor = factor * decays[8 * d : 8 * d + 1, :]
+        factor = factor * decays_ref[8 * d : 8 * d + 1, :]
 
     def back_copy(k, owner):
         return pltpu.make_async_remote_copy(
@@ -281,7 +286,7 @@
 
     inc_ref[own_part(place)] = back_ref[place]
 
-    loads[2].wait()
+    loads[9].wait()
 
     @pl.loop(1, line)
     def _(k):
@@ -345,19 +350,23 @@
         )
 
     ahead, behind = (me + n_head - 1) % n_head, (me + 1) % n_head
-    finish(ahead)
-
-    @pl.loop(0, parts)
-    def _(j):
+    def first_right(j):
         send_r[0, j] = product(ahead, j * cut).astype(BF16)
         right_copy(0, j).start()
 
-    finish(behind)
-
-    @pl.loop(0, parts)
-    def _(j):
+    def first_left(j):
         send_l[0, j] = product(behind, out_width // 2 + j * cut).astype(BF16)
         left_copy(0, j).start()
+
+    finish(ahead)
+    first_right(0)
+    finish(behind)
+    first_left(0)
+
+    @pl.loop(1, parts)
+    def _(j):
+        first_right(j)
+        first_left(j)
 
     for k in range(2, n_head):
         finish((me + k) % n_head) if k < n_head - 1 else finish(me)
@@ -425,26 +434,32 @@
     out_width = w_out.shape[1]
     state_size = b_in.shape[1] * n_head
     spans = rows // SPAN
-    bc = jnp.concatenate([b_in, c_in], axis=1).T
     part, half = state_size * 2 // line, width // 2
     parts = 5
     cut = out_width // 2 // parts
     ring = (n_head - 1, parts, rows // n_head, cut)
     vmem, anywhere = pl.BlockSpec(memory_space=pltpu.VMEM), pl.BlockSpec(memory_space=pl.ANY)
     dma = pltpu.SemaphoreType.DMA
-    return pl.pallas_call(
+    result = pl.pallas_call(
         functools.partial(layer_kernel, sizes),
-        out_shape=jax.ShapeDtypeStruct((rows // n_head, out_width), BF16),
-        in_specs=[vmem] * 6 + [anywhere] * 3,
+        out_shape=pltpu.VMEM((rows // n_head, out_width), BF16),
+        in_specs=[anywhere] * 10,
         out_specs=vmem,
         scratch_shapes=[
+            pltpu.VMEM((state_size // n_head, rows), BF16),
+            pltpu.VMEM((state_size // n_head, rows), BF16),
+            pltpu.VMEM((heads, rows), F32),
+            pltpu.VMEM((1, heads), F32),
+            pltpu.VMEM((1, heads), F32),
+            pltpu.VMEM((1, width), F32),
+            pltpu.VMEM((1, doc_lengths.shape[0]), jnp.int32),
             pltpu.VMEM((rows, width), BF16),
             pltpu.VMEM((rows, width), BF16),
             pltpu.VMEM(w_out.shape, BF16),
             pltpu.VMEM((state_size, rows), BF16),
             pltpu.VMEM((state_size, rows), BF16),
             pltpu.VMEM((rows, width), BF16),
-            pltpu.VMEM((rows, heads), F32),
+            pltpu.VMEM((heads, rows), F32),
             pltpu.VMEM((spans * 16, width), F32),
             pltpu.VMEM((spans, state_size, width), F32),
             pltpu.VMEM((rows, width), F32),
@@ -464,7 +479,8 @@
             pltpu.VMEM(ring, BF16),
             pltpu.VMEM(ring, BF16),
             pltpu.VMEM(ring, BF16),
-            dma((3,)),
+            pltpu.VMEM((line * 8, half), F32),
+            dma((10,)),
             dma((2, n_head)),
             dma((2, n_head)),
             dma((line,)),
@@ -487,8 +503,9 @@
         ),
         name="ssd_layer",
     )(
-        bc,
-        dt_raw,
+        b_in.T,
+        c_in.T,
+        dt_raw.T,
         decay_rate[None, :],
         skip_gain[None, :],
         norm_gain[None, :],
@@ -497,6 +514,7 @@
         z_gate,
         w_out,
     )
+    return result
 
 
 def solution(mesh):

time: 94.2 us -> 86 us (0.913)
  local copies, waits for them, and re-layouts: 4.29 us -> 1.06 us
  Pallas kernels: 88.1 us -> 84.9 us
  other arithmetic: 1.52 us -> 0 us
    pallas_call x1, Pallas kernels: 88.1 us -> 84.9 us  [on_device(): pl.pallas_call(functools.partial(layer_kernel, sizes), out_shape=pltpu.VM...]
    unnamed x2 -> x1, local copies, waits for them, and re-layouts: 4.29 us -> 1.06 us
    transpose x1 -> x0, other arithmetic: 1.52 us -> none  [on_device(): bc = jnp.concatenate([b_in, c_in], axis=1).T]
where the time goes in v4:
time: 86 us; the launch traced here: 85.9 us
  Pallas kernels  84.9 us (99%)
  local copies, waits for them, and re-layouts  1.06 us (1%)
    pallas_call x1, Pallas kernels, on_device(): pl.pallas_call(functools.partial(layer_kernel, sizes), out_shape=pltpu.VM...  84.9 us

profile of v4, /device:TPU:1, one launch (start us, length us, event | category | flops | bytes accessed | tf_op | source)
XLA Modules:
  0.0 85.9 jit_solution(854201372145325446)
XLA Ops:
  0.0 84.9 %ssd_layer.1 = bf16[256,2560]{1,0:T(8,128)(2,1)S(1)} custom-call(bf16[32,1024]{1,0:T(8,128)(2,1)} %bitcast.7, bf16[32,1024]{1,0:T(8,128)(2,1)} %bitcast.8, f32[16,1024]{1,0:T(8,128)} %bitcast.9, f32[1,16]{1,0:T(1,128)} %bitcast.11, f32[1,16]{1,0:T(1,128)} %bitcast.12, f32[1,1024]{1,0:T(1,128)} %bitcast.10, s32[1,32]{1,0:T(1,128)} %bitcast.13, ...), custom_call_target="tpu_custom_call" | custom-call | tf_op jit(solution)/shard_map/ssd_layer/pallas_call | solution.py:443
  84.9 1.1 %copy.12 = bf16[256,2560]{1,0:T(8,128)(2,1)} copy(bf16[256,2560]{1,0:T(8,128)(2,1)S(1)} %ssd_layer.1) | data formatting | bytes 2621440

commit v5 on v4

--- a/solution.py
+++ b/solution.py
@@ -41,7 +41,7 @@
     out_ref,
     b_ref, c_ref, dt_ref, rate_ref, skip_ref, gain_ref, docs_ref, x_ref, z_ref, w_ref, bt_ref, ct_ref, xf_ref, e_ref, rows_ref, before_ref, ur_ref, as_ref,
     state_ref, decay_ref, got_state, got_decay, line_ref, got_line, back_ref, inc_ref, norm_ref,
-    sq_ref, got_sq, send_r, got_r, send_l, got_l, decays_ref,
+    sq_ref, got_sq, send_r, got_r, send_l, got_l, decays_ref, cn_ref, folded_ref, own_state_ref,
     in_sem, bc_send, bc_recv, st_send, st_recv, dc_send, dc_recv, ln_send, ln_recv, bk_send, bk_recv,
     sq_send, sq_recv, r_send, r_recv, l_send, l_recv,
 ):
@@ -95,7 +95,7 @@
         )
 
     for what in range(2):
-        for k in range(1, n_head):
+        for k in (2, 1, n_head - 1):
             bc_copy(k, what, me).start()
         mine = pl.ds(pl.multiple_of(me * piece, piece), piece)
         (bt_ref, ct_ref)[what][mine, :] = (b_ref, c_ref)[what][...]
@@ -152,6 +152,9 @@
     decay_ref[...] = jnp.zeros_like(decay_ref)
     decay_ref[:, :heads] = jnp.broadcast_to(device_decay, (heads, 128)).T[:8, :]
 
+    def farthest_first(i):
+        return line // 2 + jnp.where(i % 2 == 0, i // 2, -(i // 2))
+
     def line_peer(k):
         return {"seq": first + (place + k) % line}
 
@@ -207,8 +210,8 @@
         )
 
     @pl.loop(1, line)
-    def _(k):
-        state_copy(k, place).start()
+    def _(i):
+        state_copy(farthest_first(i), place).start()
 
     got_state[place] = state_ref[own_part(place)]
 
@@ -219,6 +222,55 @@
     lanes = iota((128, half), 1) + (place % 2) * half
     spread_here = (lanes // head_size == iota((128, half), 0)).astype(BF16)
     decays_ref[...] = expand(got_decay[...].reshape(line * 8, 128).T, spread_here, 3)
+    @pl.loop(1, line)
+    def _(k):
+        state_copy(k, from_peer(k)).wait_recv()
+
+    inside, inc = [], jnp.zeros((part, half), F32)
+    for d in range(line):
+        inside.append(inc)
+        inc = decays_ref[8 * d : 8 * d + 1, :] * inc + got_state[d].astype(F32)
+    line_ref[...] = inc
+    line_copy = pltpu.make_async_remote_copy(
+        src_ref=line_ref,
+        dst_ref=got_line,
+        send_sem=ln_send,
+        recv_sem=ln_recv,
+        device_id={"seq": (seq + line) % n_seq},
+        device_id_type=MESH,
+    )
+    pl.when(at_line < n_seq // line - 1)(line_copy.start)
+
+    @pl.when(at_line > 0)
+    def _():
+        line_copy.wait_recv()
+
+    @pl.when(at_line == 0)
+    def _():
+        got_line[...] = jnp.zeros_like(got_line)
+
+    factor = jnp.ones((1, half), F32)
+    earlier = got_line[...]
+    for d in range(line):
+        back_ref[d] = (inside[d] + factor * earlier).astype(BF16)
+        factor = factor * decays_ref[8 * d : 8 * d + 1, :]
+
+    def back_copy(k, owner):
+        return pltpu.make_async_remote_copy(
+            src_ref=back_ref.at[(place + k) % line],
+            dst_ref=inc_ref.at[own_part(owner)],
+            send_sem=bk_send.at[k],
+            recv_sem=bk_recv.at[owner],
+            device_id=line_peer(k),
+            device_id_type=MESH,
+        )
+
+    @pl.loop(1, line)
+    def _(i):
+        back_copy(farthest_first(i), place).start()
+
+    inc_ref[own_part(place)] = back_ref[place]
+
     for k in range(1, n_head):
         bc_copy(k, 1, (me + n_head - k) % n_head).wait_recv()
     for one in loads[6:9]:
@@ -231,6 +283,7 @@
         at = pl.ds(pl.multiple_of(s * SPAN, SPAN), SPAN)
         col, row, previous, _ = ids_of(s)
         c_here = ct_ref[:, at].T
+        cn_ref[at, :] = c_here
         scores = jnp.dot(c_here, bt_ref[:, at], preferred_element_type=F32)
         seen = (col == row) & (iota((SPAN, SPAN), 0) >= iota((SPAN, SPAN), 1))
         scores = jnp.where(seen, scores, 0.0).astype(BF16)
@@ -245,47 +298,6 @@
         ur_ref[at, :] = y * gate
         as_ref[at, :] = out_of_middle * from_start * gate
 
-    @pl.loop(1, line)
-    def _(k):
-        state_copy(k, from_peer(k)).wait_recv()
-
-    inside, inc = [], jnp.zeros((part, half), F32)
-    for d in range(line):
-        inside.append(inc)
-        inc = decays_ref[8 * d : 8 * d + 1, :] * inc + got_state[d].astype(F32)
-    line_ref[...] = inc
-    line_copy = pltpu.make_async_remote_copy(
-        src_ref=line_ref,
-        dst_ref=got_line,
-        send_sem=ln_send,
-        recv_sem=ln_recv,
-        device_id={"seq": (seq + line) % n_seq},
-        device_id_type=MESH,
-    )
-    line_copy.start()
-    line_copy.wait_recv()
-    factor = jnp.where(at_line + iota((1, half), 0) > 0, 1.0, 0.0)
-    earlier = got_line[...]
-    for d in range(line):
-        back_ref[d] = (inside[d] + factor * earlier).astype(BF16)
-        factor = factor * decays_ref[8 * d : 8 * d + 1, :]
-
-    def back_copy(k, owner):
-        return pltpu.make_async_remote_copy(
-            src_ref=back_ref.at[(place + k) % line],
-            dst_ref=inc_ref.at[own_part(owner)],
-            send_sem=bk_send.at[k],
-            recv_sem=bk_recv.at[owner],
-            device_id=line_peer(k),
-            device_id_type=MESH,
-        )
-
-    @pl.loop(1, line)
-    def _(k):
-        back_copy(k, place).start()
-
-    inc_ref[own_part(place)] = back_ref[place]
-
     loads[9].wait()
 
     @pl.loop(1, line)
@@ -299,15 +311,18 @@
             decay = rows_ref[16 * s + 8 : 16 * s + 9, :]
             before = jnp.where(s + iota((1, width), 0) < block, before * decay, before)
         carried = (inc_ref[...].astype(F32) * before).astype(BF16)
-        inter = jnp.dot(ct_ref[:, at].T, carried, preferred_element_type=F32)
+        inter = jnp.dot(cn_ref[at, :], carried, preferred_element_type=F32)
         gated = ur_ref[at, :] + as_ref[at, :] * inter
         norm_ref[at, :] = (gated * gain_ref[...]).astype(BF16)
         squares = gated * gated
         folded = squares[:, :128]
         for j in range(1, width // 128):
             folded = folded + squares[:, 128 * j : 128 * (j + 1)]
-        row = jnp.sum(folded.T, axis=0, keepdims=True)
-        sq_ref[block] = jnp.broadcast_to(row, (8, SPAN))
+        folded_ref[at, :] = folded
+
+    def square_rows(block):
+        folded = folded_ref[pl.ds(pl.multiple_of(block * SPAN, SPAN), SPAN), :]
+        sq_ref[block] = jnp.broadcast_to(jnp.sum(folded.T, axis=0, keepdims=True), (8, SPAN))
 
     def square_copy(k, owner):
         return pltpu.make_async_remote_copy(
@@ -370,6 +385,8 @@
 
     for k in range(2, n_head):
         finish((me + k) % n_head) if k < n_head - 1 else finish(me)
+    for k in range(n_head):
+        square_rows((me + k) % n_head)
     for k in range(1, n_head):
         square_copy(k, me).start()
 
@@ -418,7 +435,7 @@
         state_copy(k, place).wait_send()
         back_copy(k, place).wait_send()
 
-    line_copy.wait_send()
+    pl.when(at_line < n_seq // line - 1)(line_copy.wait_send)
     for step in range(n_head - 1):
 
         @pl.loop(0, parts)
@@ -480,6 +497,9 @@
             pltpu.VMEM(ring, BF16),
             pltpu.VMEM(ring, BF16),
             pltpu.VMEM((line * 8, half), F32),
+            pltpu.VMEM((rows, state_size), BF16),
+            pltpu.VMEM((rows, 128), F32),
+            pltpu.VMEM((state_size // n_head, width), BF16),
             dma((10,)),
             dma((2, n_head)),
             dma((2, n_head)),

time: 86 us -> 82 us (0.953)
  the two profiles are of different devices: /device:TPU:1 before, /device:TPU:6 now
where the time goes in v5:
time: 82 us; the launch traced here: 81.9 us
  Pallas kernels  80.9 us (99%)
  local copies, waits for them, and re-layouts  1.06 us (1%)
    pallas_call x1, Pallas kernels, on_device(): pl.pallas_call(functools.partial(layer_kernel, sizes), out_shape=pltpu.VM...  80.9 us

profile of v5, /device:TPU:6, one launch (start us, length us, event | category | flops | bytes accessed | tf_op | source)
XLA Modules:
  0.0 81.9 jit_solution(15823277645806274239)
XLA Ops:
  0.0 80.9 %ssd_layer.1 = bf16[256,2560]{1,0:T(8,128)(2,1)S(1)} custom-call(bf16[32,1024]{1,0:T(8,128)(2,1)} %bitcast.7, bf16[32,1024]{1,0:T(8,128)(2,1)} %bitcast.8, f32[16,1024]{1,0:T(8,128)} %bitcast.9, f32[1,16]{1,0:T(1,128)} %bitcast.11, f32[1,16]{1,0:T(1,128)} %bitcast.12, f32[1,1024]{1,0:T(1,128)} %bitcast.10, s32[1,32]{1,0:T(1,128)} %bitcast.13, ...), custom_call_target="tpu_custom_call" | custom-call | tf_op jit(solution)/shard_map/ssd_layer/pallas_call | solution.py:460
  80.9 1.1 %copy.12 = bf16[256,2560]{1,0:T(8,128)(2,1)} copy(bf16[256,2560]{1,0:T(8,128)(2,1)S(1)} %ssd_layer.1) | data formatting | bytes 2621440

commit v6 on v5

--- a/solution.py
+++ b/solution.py
@@ -41,7 +41,7 @@
     out_ref,
     b_ref, c_ref, dt_ref, rate_ref, skip_ref, gain_ref, docs_ref, x_ref, z_ref, w_ref, bt_ref, ct_ref, xf_ref, e_ref, rows_ref, before_ref, ur_ref, as_ref,
     state_ref, decay_ref, got_state, got_decay, line_ref, got_line, back_ref, inc_ref, norm_ref,
-    sq_ref, got_sq, send_r, got_r, send_l, got_l, decays_ref, cn_ref, folded_ref, own_state_ref,
+    sq_ref, got_sq, send_r, got_r, send_l, got_l, decays_ref, cn_ref, folded_ref, kept_ref,
     in_sem, bc_send, bc_recv, st_send, st_recv, dc_send, dc_recv, ln_send, ln_recv, bk_send, bk_recv,
     sq_send, sq_recv, r_send, r_recv, l_send, l_recv,
 ):
@@ -180,17 +180,22 @@
     for k in range(1, n_head):
         bc_copy(k, 0, (me + n_head - k) % n_head).wait_recv()
 
-    def state_span(s, running):
-        at = pl.ds(pl.multiple_of(s * SPAN, SPAN), SPAN)
-        before_ref[s] = running
+    for s in range(spans):
         _, row, _, last = ids_of(s)
-        kept = jnp.where(row == last, bt_ref[:, at].astype(F32), 0.0).astype(BF16)
-        sums = jnp.dot(kept, xf_ref[at, :], preferred_element_type=F32)
-        base = pl.multiple_of(s * 16, 16)
-        return rows_ref[pl.ds(base + 8, 1), :] * running + sums * rows_ref[pl.ds(base, 1), :]
-
-    final = lax.fori_loop(0, spans, state_span, jnp.zeros((state_size, width), F32))
-    state_ref[...] = final.astype(BF16)
+        at = slice(s * SPAN, (s + 1) * SPAN)
+        kept_ref[:, at] = jnp.where(row == last, bt_ref[:, at].astype(F32), 0.0).astype(BF16)
+
+    @pl.loop(0, width // SPAN)
+    def _(n):
+        lanes_here = pl.ds(pl.multiple_of(n * SPAN, SPAN), SPAN)
+        running = jnp.zeros((state_size, SPAN), F32)
+        for s in range(spans):
+            at = slice(s * SPAN, (s + 1) * SPAN)
+            before_ref[s, :, lanes_here] = running
+            sums = jnp.dot(kept_ref[:, at], xf_ref[at, lanes_here], preferred_element_type=F32)
+            to_last = rows_ref[16 * s : 16 * s + 1, lanes_here]
+            running = rows_ref[16 * s + 8 : 16 * s + 9, lanes_here] * running + sums * to_last
+        state_ref[:, lanes_here] = running.astype(BF16)
 
     def own_part(t):
         return (
@@ -499,7 +504,7 @@
             pltpu.VMEM((line * 8, half), F32),
             pltpu.VMEM((rows, state_size), BF16),
             pltpu.VMEM((rows, 128), F32),
-            pltpu.VMEM((state_size // n_head, width), BF16),
+            pltpu.VMEM((state_size, rows), BF16),
             dma((10,)),
             dma((2, n_head)),
             dma((2, n_head)),

time: 82 us -> 81.8 us (level)
  no operation moved by 1% of the time
where the time goes in v6:
time: 81.8 us; the launch traced here: 81.7 us
  Pallas kernels  80.7 us (99%)
  local copies, waits for them, and re-layouts  1.06 us (1%)
    pallas_call x1, Pallas kernels, on_device(): pl.pallas_call(functools.partial(layer_kernel, sizes), out_shape=pltpu.VM...  80.7 us

profile of v6, /device:TPU:6, one launch (start us, length us, event | category | flops | bytes accessed | tf_op | source)
XLA Modules:
  0.0 81.7 jit_solution(18373476409375140649)
XLA Ops:
  0.0 80.7 %ssd_layer.1 = bf16[256,2560]{1,0:T(8,128)(2,1)S(1)} custom-call(bf16[32,1024]{1,0:T(8,128)(2,1)} %bitcast.7, bf16[32,1024]{1,0:T(8,128)(2,1)} %bitcast.8, f32[16,1024]{1,0:T(8,128)} %bitcast.9, f32[1,16]{1,0:T(1,128)} %bitcast.11, f32[1,16]{1,0:T(1,128)} %bitcast.12, f32[1,1024]{1,0:T(1,128)} %bitcast.10, s32[1,32]{1,0:T(1,128)} %bitcast.13, ...), custom_call_target="tpu_custom_call" | custom-call | tf_op jit(solution)/shard_map/ssd_layer/pallas_call | solution.py:465
  80.7 1.1 %copy.12 = bf16[256,2560]{1,0:T(8,128)(2,1)} copy(bf16[256,2560]{1,0:T(8,128)(2,1)S(1)} %ssd_layer.1) | data formatting | bytes 2621440
